TPU v7x, 32 devices: a whole 2x2x4 slice. The times are simulated.
32 devices in a mesh: beam: 2 (over x), tm: 16 (over z, y, core).
Axes of the slice: x: 2, y: 2, z: 4, core: 2. Of those that a mesh axis runs over, the one named last changes fastest.
Arguments:
- voltage: bfloat16 [2, 2, 2097152], P(None, None, ('beam', 'tm')), parts along dimension 2, may hold values from -11 to 11
- delays: int32 [64, 2048], replicated, may hold values from 0 to 96, as said below
- chan_mask: int32 [4096], P('beam'), parts along dimension 0, may hold values 0 or 1
Outputs:
- zscore: float32 [64, 1024], P(None, ('beam', 'tm')), parts along dimension 1
- trial_stats: float32 [3, 128], P(None, 'beam'), parts along dimension 1
There are 2 independent parts, one for each index of `beam`. A program takes and returns all parts, laid end to end along the dimension named above; an argument that names none is the same for every part. Nothing has to cross between parts.
Inputs may be any that keep to these rules, and one draw needn't show every extreme that they name: For each trial the delays never rise from one channel to the next; the last channel's delays are 0, and the first channel's delay of some trial is 96.
All inputs are finite; a program needn't handle non-finite values.
Results may differ from a plain program's by a relative error of at most 0.002.
Values may be sent and summed in bfloat16 or wider, within the bound.
A program may use at most 64 MiB of HBM per device.

v0:
```python
import functools
import math

import jax
import jax.numpy as jnp
import numpy as np
from jax import lax
from jax.experimental import pallas as pl
from jax.experimental.pallas import tpu as pltpu
from jax.sharding import PartitionSpec as P

NCHAN = 2048
TAPS = 16
DSPAN = 3
LANES = 128
RADIX = NCHAN // LANES
STEP = 9
GRANT = 16 * 1024 * 1024
MESH = pl.DeviceIdType.MESH


def prototype():
    length = TAPS * NCHAN
    position = np.arange(length, dtype=np.float64)
    window = 0.54 - 0.46 * np.cos(2.0 * np.pi * position / (length - 1))
    shaped = np.sinc((position - (length - 1) / 2.0) / NCHAN) * window
    shaped = shaped * np.sqrt(NCHAN / np.sum(shaped * shaped))
    taps = shaped.reshape(TAPS, RADIX, 1, LANES)
    taps = np.broadcast_to(taps, (TAPS, RADIX, 2, LANES))
    return taps.reshape(TAPS, 2 * RADIX, LANES).astype(np.float32)


def twiddles():
    angle = -2.0 * np.pi * np.outer(np.arange(RADIX), np.arange(LANES)) / NCHAN
    return np.stack([np.cos(angle), np.sin(angle)]).astype(np.float32)


def transform_table():
    angle = -2.0 * np.pi * (np.outer(np.arange(LANES), np.arange(LANES)) % LANES) / LANES
    scale = 1.0 / math.sqrt(NCHAN)
    cos, sin = np.cos(angle) * scale, np.sin(angle) * scale
    full = np.block([[cos, sin], [-sin, cos]]).astype(np.float32)
    high = full.astype(jnp.bfloat16)
    low = (full - high.astype(np.float32)).astype(jnp.bfloat16)
    return np.stack([high, low])


def butterflies(items):
    count = len(items)
    if count == 1:
        return items
    even = butterflies(items[0::2])
    odd = butterflies(items[1::2])
    half = count // 2
    out = [None] * count
    for k in range(half):
        re, im = odd[k]
        if k == 0:
            tr, ti = re, im
        elif 4 * k == count:
            tr, ti = im, -re
        elif 8 * k == count:
            r = math.sqrt(0.5)
            tr, ti = (re + im) * r, (im - re) * r
        elif 8 * k == 3 * count:
            r = math.sqrt(0.5)
            tr, ti = (im - re) * r, (re + im) * (-r)
        else:
            c, s = math.cos(2 * math.pi * k / count), -math.sin(2 * math.pi * k / count)
            tr, ti = re * c - im * s, re * s + im * c
        er, ei = even[k]
        out[k] = (er + tr, ei + ti)
        out[k + half] = (er - tr, ei - ti)
    return out


def channelize_kernel(count, frames, volt_ref, taps_ref, twid_ref, table_ref, delay_ref, mask_ref, out_ref,
                      relative_ref, meta_ref, halo, ext, weighted, sections, energy, power, send_sem, recv_sem):
    me = lax.axis_index("tm")
    past = TAPS - 1
    lines = 2 * RADIX
    half = frames // 2
    quarter = frames // 4
    cut = min(quarter, past - 1)
    spans = ((cut, past - cut), (0, cut))
    barrier = pltpu.get_barrier_semaphore()

    def pass_on(i):
        begin, size = spans[i]
        return pltpu.make_async_remote_copy(
            src_ref=volt_ref.at[:, pl.ds(frames - past + begin, size)],
            dst_ref=halo.at[:, pl.ds(begin, size)],
            send_sem=send_sem.at[i],
            recv_sem=recv_sem.at[i],
            device_id={"tm": me + 1},
            device_id_type=MESH,
        )

    @pl.when(me > 0)
    def _():
        pl.semaphore_signal(barrier, inc=1, device_id={"tm": me - 1}, device_id_type=MESH)

    @pl.when(me < count - 1)
    def _():
        pl.semaphore_wait(barrier, 1)
        pass_on(0).start()
        pass_on(1).start()

    for p in range(2):
        ext[p, past:past + frames] = volt_ref[p].astype(jnp.float32)

    def fir(begin, end):
        for part in range(lines // 8):
            rows = pl.ds(8 * part, 8)
            taps = [taps_ref[j, rows, :] for j in range(TAPS)]

            def one(f, carry):
                for p in range(2):
                    terms = [taps[j] * ext[p, f + j, rows, :] for j in range(TAPS)]
                    while len(terms) > 1:
                        terms = [a + b for a, b in zip(terms[0::2], terms[1::2])]
                    start = pl.multiple_of((p * frames + f) * lines, 8) + 8 * part
                    weighted[pl.ds(start, 8), :] = terms[0]
                return carry

            lax.fori_loop(begin, end, one, 0, unroll=4)

    def transform(begin, size):
        group = 8
        rows_half = 2 * size
        for g in range(rows_half // group):
            p, f = divmod(g * group, size)
            first = (p * frames + begin + f) * lines
            items = []
            for m in range(RADIX):
                re = weighted[pl.ds(first + 2 * m, group, stride=lines), :]
                im = weighted[pl.ds(first + 2 * m + 1, group, stride=lines), :]
                items.append((re, im))
            for k1, (re, im) in enumerate(butterflies(items)):
                if k1:
                    c, s = twid_ref[0, k1:k1 + 1, :], twid_ref[1, k1:k1 + 1, :]
                    re, im = re * c - im * s, re * s + im * c
                place = k1 * rows_half + g * group
                sections[place:place + group, :LANES] = re
                sections[place:place + group, LANES:] = im
        both = sections[0:RADIX * rows_half, :]
        high = both.astype(jnp.bfloat16)
        low = (both - high.astype(jnp.float32)).astype(jnp.bfloat16)
        dot = functools.partial(jnp.dot, preferred_element_type=jnp.float32)
        spec = dot(high, table_ref[0]) + (dot(high, table_ref[1]) + dot(low, table_ref[0]))
        spec = spec * spec
        both_pols = (spec[:, :LANES] + spec[:, LANES:]).reshape(RADIX, 2, size, LANES)
        energy[:, begin:begin + size, :] = both_pols[:, 0] + both_pols[:, 1]

    fir(half, frames)
    transform(half, frames - half)
    trials = delay_ref.shape[0]
    blocks = NCHAN // LANES
    lane = lax.broadcasted_iota(jnp.int32, (trials, LANES), 1)
    meta = jnp.zeros((trials, LANES), jnp.int32)
    most = jnp.zeros((trials, 1), jnp.int32)
    for b in range(blocks):
        block = delay_ref[:, b * LANES:(b + 1) * LANES]
        base = block[:, LANES - 1:LANES]
        away = block - base
        most = jnp.maximum(most, away[:, 0:1])
        meta = jnp.where(lane == b, base, meta)
        away = jnp.where(mask_ref[b:b + 1, :] > 0, away, -1)
        relative_ref[:, b * LANES:(b + 1) * LANES] = away.astype(jnp.float32).astype(jnp.bfloat16)
    meta_ref[...] = jnp.where(lane == blocks, most, meta)

    for i, (begin, end) in enumerate(((quarter, half), (0, quarter))):
        first, size = spans[i]

        @pl.when(me > 0)
        def _():
            pass_on(i).wait_recv()
            for p in range(2):
                ext[p, first:first + size] = halo[p, first:first + size].astype(jnp.float32)

        @pl.when(me == 0)
        def _():
            for p in range(2):
                ext[p, first:first + size] = jnp.zeros((size, lines, LANES), jnp.float32)

        fir(begin, end)
        transform(begin, end - begin)

    for k1 in range(RADIX):
        padded = jnp.concatenate([jnp.zeros((LANES - frames, LANES), jnp.float32), energy[k1]], axis=0)
        power[pl.ds(k1, LANES, stride=RADIX), :] = padded.T
    out_ref[...] = power[...].astype(jnp.bfloat16)

    @pl.when(me < count - 1)
    def _():
        pass_on(0).wait_send()
        pass_on(1).wait_send()


def dedisperse_kernel(frames, relative, meta_ref, power_ref, out_ref, acc):
    trials = relative.shape[0]
    blocks = NCHAN // LANES
    most = meta_ref[:, blocks:blocks + 1]
    zeros = jnp.zeros((LANES, LANES), jnp.bfloat16)

    def sweep(first, pair):
        upper = power_ref[2 * pair * LANES:(2 * pair + 1) * LANES, :]
        lower = power_ref[(2 * pair + 1) * LANES:(2 * pair + 2) * LANES, :]
        values = jnp.concatenate(
            [jnp.concatenate([upper, zeros], axis=1), jnp.concatenate([zeros, lower], axis=1)], axis=0
        )
        away = relative[:, 2 * pair * LANES:(2 * pair + 2) * LANES]
        picks = []
        for r in range(STEP):
            target = jnp.asarray(first + r, jnp.float32).astype(jnp.bfloat16)
            picks.append(jnp.where(away == target, jnp.ones_like(away), jnp.zeros_like(away)))
        sums = jnp.dot(jnp.concatenate(picks, axis=0), values, preferred_element_type=jnp.float32)
        out = []
        for side in range(2):
            part = sums[:, side * LANES:(side + 1) * LANES]
            run = part[:trials]
            for r in range(1, STEP):
                run = run + pltpu.roll(part[r * trials:(r + 1) * trials], LANES - r, 1)
            out.append(run)
        return out

    for pair in range(blocks // 2):
        for side, run in enumerate(sweep(0, pair)):
            acc[2 * pair + side] = run

    def more(i, carry):
        first = i * STEP
        turn = lax.rem(2 * LANES - first, LANES)
        for pair in range(blocks // 2):
            for side, run in enumerate(sweep(first, pair)):
                acc[2 * pair + side] += pltpu.roll(run, turn, 1)
        return carry

    lax.fori_loop(1, lax.div(jnp.max(most), STEP) + 1, more, 0)
    lane = lax.broadcasted_iota(jnp.int32, (trials, LANES), 1)
    total = jnp.zeros((trials, LANES), jnp.float32)
    for b in range(blocks):
        place = (lane + meta_ref[:, b:b + 1]) & (LANES - 1)
        total = total + jnp.take_along_axis(acc[b], place, axis=1, mode="promise_in_bounds")
    turned = jnp.concatenate([total, jnp.zeros((LANES - trials, LANES), jnp.float32)], axis=0).T
    half = frames // 2
    for s in range(LANES // frames):
        top = turned[s * frames:s * frames + half]
        low = turned[s * frames + half:(s + 1) * frames]
        out_ref[s * half:(s + 1) * half, :] = top + pltpu.roll(low, trials, 1)


def combine_kernel(count, frames, part_ref, mask_ref, z_ref, stats_ref, landed, mine, gathered, near_send, near_recv,
                   far_send, far_recv):
    me = lax.axis_index("tm")
    half = frames // 2
    trials = LANES // 2
    barrier = pltpu.get_barrier_semaphore()
    for k in range(1, count):
        pl.semaphore_signal(barrier, inc=1, device_id={"tm": lax.rem(me + k, count)}, device_id_type=MESH)
    pl.semaphore_wait(barrier, count - 1)

    def near(k):
        return pltpu.make_async_remote_copy(
            src_ref=part_ref.at[pl.ds((DSPAN - k) * half, half)],
            dst_ref=landed.at[k - 1],
            send_sem=near_send.at[k - 1],
            recv_sem=near_recv.at[k - 1],
            device_id={"tm": me - k},
            device_id_type=MESH,
        )

    for k in range(1, DSPAN + 1):
        @pl.when(me >= k)
        def _():
            near(k).start()

    series = part_ref[DSPAN * half:(DSPAN + 1) * half, :]
    for k in range(1, DSPAN + 1):
        @pl.when(me + k >= count)
        def _():
            landed[k - 1] = jnp.zeros((half, LANES), jnp.float32)

        @pl.when(me + k < count)
        def _():
            near(k).wait_recv()
    for k in range(1, DSPAN + 1):
        series = series + landed[k - 1]

    def fold(value, op):
        return op(value, pltpu.roll(value, trials, 1))

    mean = fold(jnp.sum(series, axis=0, keepdims=True), jnp.add) * (1.0 / frames)
    away = series - mean
    spread = fold(jnp.sum(away * away, axis=0, keepdims=True), jnp.add)
    peak = fold(jnp.max(series, axis=0, keepdims=True), jnp.maximum)
    mine[...] = jnp.concatenate([mean, spread, peak, jnp.zeros((5, LANES), jnp.float32)], axis=0)

    def far(k):
        return pltpu.make_async_remote_copy(
            src_ref=mine,
            dst_ref=gathered.at[k - 1],
            send_sem=far_send.at[k - 1],
            recv_sem=far_recv.at[k - 1],
            device_id={"tm": lax.rem(me + k, count)},
            device_id_type=MESH,
        )

    for k in range(1, count):
        far(k).start()
    live = jnp.maximum(jnp.sum(mask_ref[...].astype(jnp.float32)), 1.0)
    for k in range(1, count):
        far(k).wait_recv()
    everyone = gathered[...]
    average = (mean + jnp.sum(everyone[:, 0:1, :], axis=0)) * (1.0 / count)
    offset = everyone[:, 0:1, :] - average[None]
    squares = spread + jnp.sum(everyone[:, 1:2, :], axis=0)
    between = (mean - average) * (mean - average) + jnp.sum(offset * offset, axis=0)
    variance = (squares + frames * between) * (1.0 / (frames * count))
    top = jnp.maximum(peak, jnp.max(everyone[:, 2:3, :], axis=0))
    deviation = jnp.sqrt(variance + 1e-05)
    z = (series - average) / deviation
    z_ref[0:half, :] = z[:, :trials]
    z_ref[half:frames, :] = pltpu.roll(z, trials, 1)[:, :trials]
    stats_ref[...] = jnp.concatenate(
        [average / live, deviation / live, (top - average) / deviation], axis=0
    )[:, :trials]
    for k in range(1, DSPAN + 1):
        @pl.when(me >= k)
        def _():
            near(k).wait_send()
    for k in range(1, count):
        far(k).wait_send()


def per_device(voltage, delays, chan_mask):
    frames = voltage.shape[2] // NCHAN
    trials = delays.shape[0]
    count = lax.axis_size("tm")
    vmem = pl.BlockSpec(memory_space=pltpu.VMEM)
    lines = 2 * RADIX
    framed = voltage.reshape(2, 2, frames * RADIX, LANES).transpose(0, 2, 1, 3).reshape(2, frames, lines, LANES)
    mask_table = chan_mask.reshape(RADIX, LANES)
    power, relative, meta = pl.pallas_call(
        functools.partial(channelize_kernel, count, frames),
        out_shape=(
            jax.ShapeDtypeStruct((NCHAN, LANES), jnp.bfloat16),
            jax.ShapeDtypeStruct((trials, NCHAN), jnp.bfloat16),
            jax.ShapeDtypeStruct((trials, LANES), jnp.int32),
        ),
        in_specs=[vmem] * 6,
        out_specs=(vmem,) * 3,
        scratch_shapes=[
            pltpu.VMEM((2, TAPS - 1, lines, LANES), jnp.bfloat16),
            pltpu.VMEM((2, frames + TAPS - 1, lines, LANES), jnp.float32),
            pltpu.VMEM((2 * frames * lines, LANES), jnp.float32),
            pltpu.VMEM((RADIX * frames, 2 * LANES), jnp.float32),
            pltpu.VMEM((RADIX, frames, LANES), jnp.float32),
            pltpu.VMEM((NCHAN, LANES), jnp.float32),
            pltpu.SemaphoreType.DMA((2,)),
            pltpu.SemaphoreType.DMA((2,)),
        ],
        compiler_params=pltpu.CompilerParams(collective_id=1, vmem_limit_bytes=GRANT, has_side_effects=True),
        name="channelize",
    )(framed, jnp.asarray(prototype()), jnp.asarray(twiddles()), jnp.asarray(transform_table()), delays, mask_table)
    partial = pl.pallas_call(
        functools.partial(dedisperse_kernel, frames),
        out_shape=jax.ShapeDtypeStruct((2 * frames, LANES), jnp.float32),
        in_specs=[vmem] * 3,
        out_specs=vmem,
        scratch_shapes=[
            pltpu.VMEM((NCHAN // LANES, trials, LANES), jnp.float32),
        ],
        compiler_params=pltpu.CompilerParams(vmem_limit_bytes=GRANT),
        name="dedisperse",
    )(relative, meta, power)
    zscore, trial_stats = pl.pallas_call(
        functools.partial(combine_kernel, count, frames),
        out_shape=(
            jax.ShapeDtypeStruct((frames, trials), jnp.float32),
            jax.ShapeDtypeStruct((3, trials), jnp.float32),
        ),
        in_specs=[vmem] * 2,
        out_specs=(vmem, vmem),
        scratch_shapes=[
            pltpu.VMEM((DSPAN, frames // 2, LANES), jnp.float32),
            pltpu.VMEM((8, LANES), jnp.float32),
            pltpu.VMEM((count - 1, 8, LANES), jnp.float32),
            pltpu.SemaphoreType.DMA((DSPAN,)),
            pltpu.SemaphoreType.DMA((DSPAN,)),
            pltpu.SemaphoreType.DMA((count - 1,)),
            pltpu.SemaphoreType.DMA((count - 1,)),
        ],
        compiler_params=pltpu.CompilerParams(collective_id=0, vmem_limit_bytes=GRANT, has_side_effects=True),
        name="combine",
    )(partial, mask_table)
    return (zscore.T, trial_stats)


def solution(mesh):
    in_specs = (P(None, None, ("beam", "tm")), P(), P("beam"))
    out_specs = (P(None, ("beam", "tm")), P(None, "beam"))
    return jax.shard_map(
        per_device, mesh=mesh, in_specs=in_specs, out_specs=out_specs, check_vma=False
    )
```

profile of v0, /device:TPU:0, one launch (start us, length us, event | category | flops | bytes accessed | tf_op | source)
XLA Modules:
  0.0 29.3 jit_solution(3998883056904957251)
XLA Ops:
  0.6 0.0 copy-start
  0.6 1.0 %copy-done = bf16[2,2,65536]{2,1,0:T(2,128)(2,1)S(1)} copy-done((bf16[2,2,65536]{2,1,0:T(2,128)(2,1)S(1)}, bf16[2,2,65536]{2,1,0:T(2,128)(2,1)}, u32[]{:S(2)}) %copy-start) | copy-done | bytes 524312
  1.7 0.0 copy-start.1
  1.7 1.0 %copy-done.1 = s32[64,2048]{1,0:T(8,128)S(1)} copy-done((s32[64,2048]{1,0:T(8,128)S(1)}, s32[64,2048]{1,0:T(8,128)}, u32[]{:S(2)}) %copy-start.1) | copy-done | bytes 524312
  2.7 0.0 copy-start.2
  2.7 0.9 %copy-done.2 = bf16[2,256,256]{2,1,0:T(8,128)(2,1)S(1)} copy-done((bf16[2,256,256]{2,1,0:T(8,128)(2,1)S(1)}, bf16[2,256,256]{2,1,0:T(8,128)(2,1)}, u32[]{:S(2)}) %copy-start.2) | copy-done | bytes 262168
  3.7 0.0 copy-start.3
  3.7 0.9 %copy-done.3 = f32[16,32,128]{2,1,0:T(8,128)S(1)} copy-done((f32[16,32,128]{2,1,0:T(8,128)S(1)}, f32[16,32,128]{2,1,0:T(8,128)}, u32[]{:S(2)}) %copy-start.3) | copy-done | bytes 262168
  4.6 0.0 copy-start.4
  4.6 0.7 %copy-done.4 = s32[2048]{0:T(1024)S(1)} copy-done((s32[2048]{0:T(1024)S(1)}, s32[2048]{0:T(1024)}, u32[]{:S(2)}) %copy-start.4) | copy-done | bytes 8216
  5.3 0.0 copy-start.5
  5.3 0.7 %copy-done.5 = f32[2,16,128]{2,1,0:T(8,128)S(1)} copy-done((f32[2,16,128]{2,1,0:T(8,128)S(1)}, f32[2,16,128]{2,1,0:T(8,128)}, u32[]{:S(2)}) %copy-start.5) | copy-done | bytes 16408
  6.0 4.4 %channelize.1 = (bf16[2048,128]{1,0:T(8,128)(2,1)S(1)}, bf16[64,2048]{1,0:T(8,128)(2,1)S(1)}, s32[64,128]{1,0:T(8,128)S(1)}) custom-call(bf16[2,32,32,128]{3,2,1,0:T(8,128)(2,1)S(1)} %bitcast.7, f32[16,32,128]{2,1,0:T(8,128)S(1)} %copy-done.3, f32[2,16,128]{2,1,0:T(8,128)S(1)} %copy-done.5, bf16[2,256,256]{2,1,0:T(8,128)(2,1)S(1)} %copy-done.2, ...), custom_call_target="tpu_custom_call" | custom-call | tf_op jit(solution)/shard_map/channelize/pallas_call | solution.py:344
  10.4 2.8 %dedisperse.1.part_ref = f32[64,128]{1,0:T(8,128)S(1)} custom-call(bf16[64,2048]{1,0:T(8,128)(2,1)S(1)} %get-tuple-element.7.relative, s32[64,128]{1,0:T(8,128)S(1)} %get-tuple-element.8.meta_ref, bf16[2048,128]{1,0:T(8,128)(2,1)S(1)} %get-tuple-element.9.power_ref), custom_call_target="tpu_custom_call" | custom-call | tf_op jit(solution)/shard_map/dedisperse/pallas_call | solution.py:366
  13.2 14.9 %combine.1 = (f32[32,64]{1,0:T(8,128)S(1)}, f32[3,64]{1,0:T(4,128)S(1)}) custom-call(f32[64,128]{1,0:T(8,128)S(1)} %dedisperse.1.part_ref, s32[16,128]{1,0:T(8,128)S(1)} %bitcast.9), custom_call_target="tpu_custom_call" | custom-call | tf_op jit(solution)/shard_map/combine/pallas_call | solution.py:377
  28.1 0.6 %copy.11 = f32[64,32]{0,1:T(8,128)} copy(f32[64,32]{0,1:T(8,128)S(1)} %bitcast.10) | data formatting | bytes 16384
  28.7 0.6 %copy.12 = f32[3,64]{1,0:T(4,128)} copy(f32[3,64]{1,0:T(4,128)S(1)} %get-tuple-element.15) | data formatting | bytes 1536
Async XLA Ops:
  0.6 1.0 %copy-start = (bf16[2,2,65536]{2,1,0:T(2,128)(2,1)S(1)}, bf16[2,2,65536]{2,1,0:T(2,128)(2,1)}, u32[]{:S(2)}) copy-start(bf16[2,2,65536]{2,1,0:T(2,128)(2,1)} %param.6) | copy-start | bytes 1572868
  1.7 1.0 %copy-start.1 = (s32[64,2048]{1,0:T(8,128)S(1)}, s32[64,2048]{1,0:T(8,128)}, u32[]{:S(2)}) copy-start(s32[64,2048]{1,0:T(8,128)} %delay_ref.1) | copy-start | bytes 1572868
  2.7 0.9 %copy-start.2 = (bf16[2,256,256]{2,1,0:T(8,128)(2,1)S(1)}, bf16[2,256,256]{2,1,0:T(8,128)(2,1)}, u32[]{:S(2)}) copy-start(bf16[2,256,256]{2,1,0:T(8,128)(2,1)} %constant.8.clone.table_ref) | copy-start | bytes 786436
  3.7 0.9 %copy-start.3 = (f32[16,32,128]{2,1,0:T(8,128)S(1)}, f32[16,32,128]{2,1,0:T(8,128)}, u32[]{:S(2)}) copy-start(f32[16,32,128]{2,1,0:T(8,128)} %constant.6.clone.taps_ref) | copy-start | bytes 786436
  4.6 0.7 %copy-start.4 = (s32[2048]{0:T(1024)S(1)}, s32[2048]{0:T(1024)}, u32[]{:S(2)}) copy-start(s32[2048]{0:T(1024)} %param.8) | copy-start | bytes 24580
  5.3 0.7 %copy-start.5 = (f32[2,16,128]{2,1,0:T(8,128)S(1)}, f32[2,16,128]{2,1,0:T(8,128)}, u32[]{:S(2)}) copy-start(f32[2,16,128]{2,1,0:T(8,128)} %constant.7.clone.twid_ref) | copy-start | bytes 49156
where the time goes:
time: 29.6 us; the launch traced here: 29.3 us
  Pallas kernels  22 us (74%)
  local copies, waits for them, and re-layouts  6.57 us (22%)
  between operations  0.67 us (2%)
    pallas_call x1, Pallas kernels, per_device(): pl.pallas_call(functools.partial(combine_kernel, count, frames), out_shap...  14.9 us
    unnamed x14, local copies, waits for them, and re-layouts  6.57 us
    pallas_call x1, Pallas kernels, per_device(): pl.pallas_call(functools.partial(channelize_kernel, count, frames), out_s...  4.39 us
    pallas_call x1, Pallas kernels, per_device(): pl.pallas_call(functools.partial(dedisperse_kernel, frames), out_shape=ja...  2.76 us

commit v1 on v0

--- a/solution.py
+++ b/solution.py
@@ -74,8 +74,9 @@
     return out
 
 
-def channelize_kernel(count, frames, volt_ref, taps_ref, twid_ref, table_ref, delay_ref, mask_ref, out_ref,
-                      relative_ref, meta_ref, halo, ext, weighted, sections, energy, power, send_sem, recv_sem):
+def channelize_kernel(count, frames, volt_hbm, taps_hbm, twid_hbm, table_hbm, delay_hbm, mask_hbm, out_ref,
+                      relative_ref, meta_ref, mask_out, volt_ref, taps_ref, twid_ref, table_ref, delay_ref, mask_ref,
+                      halo, ext, weighted, sections, energy, power, load_sem, send_sem, recv_sem):
     me = lax.axis_index("tm")
     past = TAPS - 1
     lines = 2 * RADIX
@@ -84,6 +85,11 @@
     cut = min(quarter, past - 1)
     spans = ((cut, past - cut), (0, cut))
     barrier = pltpu.get_barrier_semaphore()
+    pairs = ((volt_hbm, volt_ref), (taps_hbm, taps_ref), (twid_hbm, twid_ref), (table_hbm, table_ref),
+             (delay_hbm, delay_ref), (mask_hbm, mask_ref))
+    loads = [pltpu.make_async_copy(a, b, load_sem.at[i]) for i, (a, b) in enumerate(pairs)]
+    for load in loads:
+        load.start()
 
     def pass_on(i):
         begin, size = spans[i]
@@ -99,6 +105,8 @@
     @pl.when(me > 0)
     def _():
         pl.semaphore_signal(barrier, inc=1, device_id={"tm": me - 1}, device_id_type=MESH)
+
+    loads[0].wait()
 
     @pl.when(me < count - 1)
     def _():
@@ -152,8 +160,14 @@
         both_pols = (spec[:, :LANES] + spec[:, LANES:]).reshape(RADIX, 2, size, LANES)
         energy[:, begin:begin + size, :] = both_pols[:, 0] + both_pols[:, 1]
 
+    loads[1].wait()
     fir(half, frames)
+    loads[2].wait()
+    loads[3].wait()
     transform(half, frames - half)
+    loads[4].wait()
+    loads[5].wait()
+    mask_out[...] = mask_ref[...]
     trials = delay_ref.shape[0]
     blocks = NCHAN // LANES
     lane = lax.broadcasted_iota(jnp.int32, (trials, LANES), 1)
@@ -161,7 +175,7 @@
     most = jnp.zeros((trials, 1), jnp.int32)
     for b in range(blocks):
         block = delay_ref[:, b * LANES:(b + 1) * LANES]
-        base = block[:, LANES - 1:LANES]
+        base = jnp.take_along_axis(block, jnp.full((trials, LANES), LANES - 1, jnp.int32), axis=1, mode="promise_in_bounds")
         away = block - base
         most = jnp.maximum(most, away[:, 0:1])
         meta = jnp.where(lane == b, base, meta)
@@ -287,14 +301,22 @@
     for k in range(1, DSPAN + 1):
         series = series + landed[k - 1]
 
+    lane = lax.broadcasted_iota(jnp.int32, (1, LANES), 1)
+
     def fold(value, op):
         return op(value, pltpu.roll(value, trials, 1))
+
+    def low_half(value):
+        return jnp.where(lane < trials, value, pltpu.roll(value, trials, 1))
+
+    def high_half(value):
+        return jnp.where(lane < trials, pltpu.roll(value, trials, 1), value)
 
     mean = fold(jnp.sum(series, axis=0, keepdims=True), jnp.add) * (1.0 / frames)
     away = series - mean
     spread = fold(jnp.sum(away * away, axis=0, keepdims=True), jnp.add)
     peak = fold(jnp.max(series, axis=0, keepdims=True), jnp.maximum)
-    mine[...] = jnp.concatenate([mean, spread, peak, jnp.zeros((5, LANES), jnp.float32)], axis=0)
+    mine[...] = jnp.concatenate([jnp.where(lane < trials, mean, spread), peak], axis=0)
 
     def far(k):
         return pltpu.make_async_remote_copy(
@@ -311,13 +333,14 @@
     live = jnp.maximum(jnp.sum(mask_ref[...].astype(jnp.float32)), 1.0)
     for k in range(1, count):
         far(k).wait_recv()
-    everyone = gathered[...]
-    average = (mean + jnp.sum(everyone[:, 0:1, :], axis=0)) * (1.0 / count)
-    offset = everyone[:, 0:1, :] - average[None]
-    squares = spread + jnp.sum(everyone[:, 1:2, :], axis=0)
-    between = (mean - average) * (mean - average) + jnp.sum(offset * offset, axis=0)
+    sums = gathered[:, 0, :]
+    tops = gathered[:, 1, :]
+    average = (mean + low_half(jnp.sum(sums, axis=0, keepdims=True))) * (1.0 / count)
+    offset = sums - average
+    squares = spread + high_half(jnp.sum(sums, axis=0, keepdims=True))
+    between = (mean - average) * (mean - average) + low_half(jnp.sum(offset * offset, axis=0, keepdims=True))
     variance = (squares + frames * between) * (1.0 / (frames * count))
-    top = jnp.maximum(peak, jnp.max(everyone[:, 2:3, :], axis=0))
+    top = jnp.maximum(peak, jnp.max(tops, axis=0, keepdims=True))
     deviation = jnp.sqrt(variance + 1e-05)
     z = (series - average) / deviation
     z_ref[0:half, :] = z[:, :trials]
@@ -333,6 +356,15 @@
         far(k).wait_send()
 
 
+def finish_kernel(z_ref, stats_ref, z_out, stats_out, sem):
+    first = pltpu.make_async_copy(z_ref, z_out, sem.at[0])
+    second = pltpu.make_async_copy(stats_ref, stats_out, sem.at[1])
+    first.start()
+    second.start()
+    first.wait()
+    second.wait()
+
+
 def per_device(voltage, delays, chan_mask):
     frames = voltage.shape[2] // NCHAN
     trials = delays.shape[0]
@@ -341,28 +373,36 @@
     lines = 2 * RADIX
     framed = voltage.reshape(2, 2, frames * RADIX, LANES).transpose(0, 2, 1, 3).reshape(2, frames, lines, LANES)
     mask_table = chan_mask.reshape(RADIX, LANES)
-    power, relative, meta = pl.pallas_call(
+    power, relative, meta, mask_table = pl.pallas_call(
         functools.partial(channelize_kernel, count, frames),
         out_shape=(
             jax.ShapeDtypeStruct((NCHAN, LANES), jnp.bfloat16),
             jax.ShapeDtypeStruct((trials, NCHAN), jnp.bfloat16),
             jax.ShapeDtypeStruct((trials, LANES), jnp.int32),
+            jax.ShapeDtypeStruct((RADIX, LANES), jnp.int32),
         ),
-        in_specs=[vmem] * 6,
-        out_specs=(vmem,) * 3,
+        in_specs=[pl.BlockSpec(memory_space=pltpu.HBM)] * 6,
+        out_specs=(vmem,) * 4,
         scratch_shapes=[
+            pltpu.VMEM((2, frames, lines, LANES), jnp.bfloat16),
+            pltpu.VMEM((TAPS, lines, LANES), jnp.float32),
+            pltpu.VMEM((2, RADIX, LANES), jnp.float32),
+            pltpu.VMEM((2, 2 * LANES, 2 * LANES), jnp.bfloat16),
+            pltpu.VMEM((trials, NCHAN), jnp.int32),
+            pltpu.VMEM((RADIX, LANES), jnp.int32),
             pltpu.VMEM((2, TAPS - 1, lines, LANES), jnp.bfloat16),
             pltpu.VMEM((2, frames + TAPS - 1, lines, LANES), jnp.float32),
             pltpu.VMEM((2 * frames * lines, LANES), jnp.float32),
             pltpu.VMEM((RADIX * frames, 2 * LANES), jnp.float32),
             pltpu.VMEM((RADIX, frames, LANES), jnp.float32),
             pltpu.VMEM((NCHAN, LANES), jnp.float32),
+            pltpu.SemaphoreType.DMA((6,)),
             pltpu.SemaphoreType.DMA((2,)),
             pltpu.SemaphoreType.DMA((2,)),
         ],
         compiler_params=pltpu.CompilerParams(collective_id=1, vmem_limit_bytes=GRANT, has_side_effects=True),
         name="channelize",
-    )(framed, jnp.asarray(prototype()), jnp.asarray(twiddles()), jnp.asarray(transform_table()), delays, mask_table)
+    )(*[pltpu.with_memory_space_constraint(v, pltpu.HBM) for v in (framed, jnp.asarray(prototype()), jnp.asarray(twiddles()), jnp.asarray(transform_table()), delays, mask_table)])
     partial = pl.pallas_call(
         functools.partial(dedisperse_kernel, frames),
         out_shape=jax.ShapeDtypeStruct((2 * frames, LANES), jnp.float32),
@@ -384,8 +424,8 @@
         out_specs=(vmem, vmem),
         scratch_shapes=[
             pltpu.VMEM((DSPAN, frames // 2, LANES), jnp.float32),
-            pltpu.VMEM((8, LANES), jnp.float32),
-            pltpu.VMEM((count - 1, 8, LANES), jnp.float32),
+            pltpu.VMEM((2, LANES), jnp.float32),
+            pltpu.VMEM((count - 1, 2, LANES), jnp.float32),
             pltpu.SemaphoreType.DMA((DSPAN,)),
             pltpu.SemaphoreType.DMA((DSPAN,)),
             pltpu.SemaphoreType.DMA((count - 1,)),
@@ -394,6 +434,18 @@
         compiler_params=pltpu.CompilerParams(collective_id=0, vmem_limit_bytes=GRANT, has_side_effects=True),
         name="combine",
     )(partial, mask_table)
+    zscore, trial_stats = pl.pallas_call(
+        finish_kernel,
+        out_shape=(
+            jax.ShapeDtypeStruct((frames, trials), jnp.float32),
+            jax.ShapeDtypeStruct((3, trials), jnp.float32),
+        ),
+        in_specs=[vmem] * 2,
+        out_specs=(pl.BlockSpec(memory_space=pltpu.HBM),) * 2,
+        scratch_shapes=[pltpu.SemaphoreType.DMA((2,))],
+        compiler_params=pltpu.CompilerParams(vmem_limit_bytes=GRANT),
+        name="finish",
+    )(zscore, trial_stats)
     return (zscore.T, trial_stats)
 
 

time: 29.6 us -> 23.7 us (0.80)
  local copies, waits for them, and re-layouts: 6.57 us -> 0 us
  Pallas kernels: 22 us -> 22.9 us
    unnamed x14 -> x0, local copies, waits for them, and re-layouts: 6.57 us -> none
    pallas_call x1, Pallas kernels: 4.39 us -> 6.08 us  [per_device(): pl.pallas_call(functools.partial(channelize_kernel, count, frames), out_s...]
    pallas_call x1, Pallas kernels: 14.9 us -> 13.4 us  [per_device(): pl.pallas_call(functools.partial(combine_kernel, count, frames), out_shap...]
    pallas_call x0 -> x1, Pallas kernels: none -> 0.63 us  [per_device(): pl.pallas_call(finish_kernel, out_shape=(jax.ShapeDtypeStruct((frames, tr...]
where the time goes in v1:
time: 23.7 us; the launch traced here: 23.5 us
  Pallas kernels  22.9 us (97%)
  between operations  0.65 us (3%)
    pallas_call x1, Pallas kernels, per_device(): pl.pallas_call(functools.partial(combine_kernel, count, frames), out_shap...  13.4 us
    pallas_call x1, Pallas kernels, per_device(): pl.pallas_call(functools.partial(channelize_kernel, count, frames), out_s...  6.08 us
    pallas_call x1, Pallas kernels, per_device(): pl.pallas_call(functools.partial(dedisperse_kernel, frames), out_shape=ja...  2.75 us
    pallas_call x1, Pallas kernels, per_device(): pl.pallas_call(finish_kernel, out_shape=(jax.ShapeDtypeStruct((frames, tr...  0.63 us

profile of v1, /device:TPU:0, one launch (start us, length us, event | category | flops | bytes accessed | tf_op | source)
XLA Modules:
  0.0 23.5 jit_solution(17280604057181454876)
XLA Ops:
  0.6 6.1 %channelize.1 = (bf16[2048,128]{1,0:T(8,128)(2,1)S(1)}, bf16[64,2048]{1,0:T(8,128)(2,1)S(1)}, s32[64,128]{1,0:T(8,128)S(1)}, s32[16,128]{1,0:T(8,128)S(1)}) custom-call(bf16[2,32,32,128]{3,2,1,0:T(8,128)(2,1)} %bitcast.7, f32[16,32,128]{2,1,0:T(8,128)} %constant.6.clone.taps_hbm, f32[2,16,128]{2,1,0:T(8,128)} %constant.7.clone.twid_hbm, ...), custom_call_target="tpu_custom_call" | custom-call | tf_op jit(solution)/shard_map/channelize/pallas_call | solution.py:376
  6.7 2.7 %dedisperse.1.part_ref = f32[64,128]{1,0:T(8,128)S(1)} custom-call(bf16[64,2048]{1,0:T(8,128)(2,1)S(1)} %get-tuple-element.10.relative, s32[64,128]{1,0:T(8,128)S(1)} %get-tuple-element.11.meta_ref, bf16[2048,128]{1,0:T(8,128)(2,1)S(1)} %get-tuple-element.12.power_ref), custom_call_target="tpu_custom_call" | custom-call | tf_op jit(solution)/shard_map/dedisperse/pallas_call | solution.py:406
  9.5 13.4 %combine.1 = (f32[32,64]{1,0:T(8,128)S(1)}, f32[3,64]{1,0:T(4,128)S(1)}) custom-call(f32[64,128]{1,0:T(8,128)S(1)} %dedisperse.1.part_ref, s32[16,128]{1,0:T(8,128)S(1)} %get-tuple-element.13.mask_ref), custom_call_target="tpu_custom_call" | custom-call | tf_op jit(solution)/shard_map/combine/pallas_call | solution.py:417
  22.9 0.6 %finish.1 = (f32[32,64]{1,0:T(8,128)}, f32[3,64]{1,0:T(4,128)}) custom-call(f32[32,64]{1,0:T(8,128)S(1)} %get-tuple-element.14.z_ref, f32[3,64]{1,0:T(4,128)S(1)} %get-tuple-element.15.stats_ref), custom_call_target="tpu_custom_call" | custom-call | tf_op jit(solution)/shard_map/finish/pallas_call | solution.py:437

commit v2 on v1

v2 whole, which is shorter than its diff:
```python
import functools
import math

import jax
import jax.numpy as jnp
import numpy as np
from jax import lax
from jax.experimental import pallas as pl
from jax.experimental.pallas import tpu as pltpu
from jax.sharding import PartitionSpec as P

NCHAN = 2048
TAPS = 16
LANES = 128
RADIX = NCHAN // LANES
MAXD = 96
EDGE = 8
HALF = MAXD // 2
GRANT = 32 * 1024 * 1024
MESH = pl.DeviceIdType.MESH


def prototype():
    length = TAPS * NCHAN
    position = np.arange(length, dtype=np.float64)
    window = 0.54 - 0.46 * np.cos(2.0 * np.pi * position / (length - 1))
    shaped = np.sinc((position - (length - 1) / 2.0) / NCHAN) * window
    shaped = shaped * np.sqrt(NCHAN / np.sum(shaped * shaped))
    taps = shaped.reshape(TAPS, RADIX, 1, LANES)
    taps = np.broadcast_to(taps, (TAPS, RADIX, 2, LANES))
    return taps.reshape(TAPS, 2 * RADIX, LANES).astype(np.float32)


def twiddles():
    angle = -2.0 * np.pi * np.outer(np.arange(RADIX), np.arange(LANES)) / NCHAN
    return np.stack([np.cos(angle), np.sin(angle)]).astype(np.float32)


def transform_table():
    angle = -2.0 * np.pi * (np.outer(np.arange(LANES), np.arange(LANES)) % LANES) / LANES
    scale = 1.0 / math.sqrt(NCHAN)
    cos, sin = np.cos(angle) * scale, np.sin(angle) * scale
    full = np.block([[cos, sin], [-sin, cos]]).astype(np.float32)
    high = full.astype(jnp.bfloat16)
    low = (full - high.astype(np.float32)).astype(jnp.bfloat16)
    return np.stack([high, low])


def butterflies(items):
    count = len(items)
    if count == 1:
        return items
    even = butterflies(items[0::2])
    odd = butterflies(items[1::2])
    half = count // 2
    out = [None] * count
    for k in range(half):
        re, im = odd[k]
        if k == 0:
            tr, ti = re, im
        elif 4 * k == count:
            tr, ti = im, -re
        elif 8 * k == count:
            r = math.sqrt(0.5)
            tr, ti = (re + im) * r, (im - re) * r
        elif 8 * k == 3 * count:
            r = math.sqrt(0.5)
            tr, ti = (im - re) * r, (re + im) * (-r)
        else:
            c, s = math.cos(2 * math.pi * k / count), -math.sin(2 * math.pi * k / count)
            tr, ti = re * c - im * s, re * s + im * c
        er, ei = even[k]
        out[k] = (er + tr, ei + ti)
        out[k + half] = (er - tr, ei - ti)
    return out


def wait_some(sem, amount):
    @pl.when(amount > 0)
    def _():
        pl.semaphore_wait(sem, amount)


def beam_kernel(count, frames, trials, volt_hbm, taps_hbm, twid_hbm, table_hbm, delay_hbm, mask_hbm, z_ref, stats_ref,
                volt_ref, taps_ref, twid_ref, table_ref, delay_ref, mask_ref, before, after, ext, weighted, sections,
                spread_out, early, late_delay, counts, picks, acc, part, landed, risen, mine, gathered,
                load_sem, halo_send, halo_recv, near_send, near_recv, far_send, far_recv, know):
    me = lax.axis_index("tm")
    past = TAPS - 1
    lead = past - EDGE
    lines = 2 * RADIX
    own = EDGE + lead
    blocks = LANES // RADIX
    wide = NCHAN // blocks
    reach = MAXD // frames
    steps = HALF + 2
    barrier = pltpu.get_barrier_semaphore()

    def here(k):
        return (me + k >= 0) & (me + k < count)

    def tell(sem, k):
        @pl.when(here(k))
        def _():
            pl.semaphore_signal(sem, inc=1, device_id={"tm": me + k}, device_id_type=MESH)

    def number(distances):
        return sum(jnp.where(here(k), 1, 0) for k in distances)

    close = [k for d in range(1, reach + 1) for k in (-d, d)]
    for k in close:
        tell(barrier, k)
    pairs = ((volt_hbm, volt_ref), (taps_hbm, taps_ref), (delay_hbm, delay_ref), (twid_hbm, twid_ref),
             (table_hbm, table_ref), (mask_hbm, mask_ref))
    loads = [pltpu.make_async_copy(a, b, load_sem.at[i]) for i, (a, b) in enumerate(pairs)]
    for load in loads:
        load.start()

    def forward():
        return pltpu.make_async_remote_copy(
            src_ref=volt_ref.at[:, pl.ds(frames - lead, lead)], dst_ref=before,
            send_sem=halo_send.at[0], recv_sem=halo_recv.at[0], device_id={"tm": me + 1}, device_id_type=MESH,
        )

    def backward():
        return pltpu.make_async_remote_copy(
            src_ref=volt_ref.at[:, pl.ds(0, EDGE)], dst_ref=after,
            send_sem=halo_send.at[1], recv_sem=halo_recv.at[1], device_id={"tm": me - 1}, device_id_type=MESH,
        )

    loads[0].wait()
    wait_some(barrier, number(close))

    @pl.when(me < count - 1)
    def _():
        forward().start()

    @pl.when(me > 0)
    def _():
        backward().start()

    rounds = []
    known = reach
    while known < count - 1:
        rounds.append(known)
        known *= 2

    def open_round(i):
        if i < len(rounds):
            for k in (-rounds[i], rounds[i]):
                tell(know.at[i], k)

    def close_round(i):
        if i < len(rounds):
            wait_some(know.at[i], number((-rounds[i], rounds[i])))

    open_round(0)
    for p in range(2):
        ext[p, own:own + frames] = volt_ref[p].astype(jnp.float32)
    for load in loads[1:]:
        load.wait()

    row = lax.broadcasted_iota(jnp.int32, (blocks, LANES), 1)
    even = mask_ref[pl.ds(0, blocks, stride=2), :]
    odd = mask_ref[pl.ds(1, blocks, stride=2), :]
    usable = []
    for h in range(2):
        place = (row & 7) * RADIX + 8 * h + row // RADIX
        low = jnp.take_along_axis(even, place, axis=1, mode="promise_in_bounds")
        high = jnp.take_along_axis(odd, place, axis=1, mode="promise_in_bounds")
        usable.append(jnp.where((row & 8) == 0, low, high).astype(jnp.float32))

    def fir(begin, size):
        for part_index in range(lines // 8):
            rows = pl.ds(8 * part_index, 8)
            taps = [taps_ref[j, rows, :] for j in range(TAPS)]

            def one(f, carry):
                for p in range(2):
                    terms = [taps[j] * ext[p, begin + EDGE + f + j, rows, :] for j in range(TAPS)]
                    while len(terms) > 1:
                        terms = [a + b for a, b in zip(terms[0::2], terms[1::2])]
                    start = pl.multiple_of((p * size + f) * lines, 8) + 8 * part_index
                    weighted[pl.ds(start, 8), :] = terms[0]
                return carry

            lax.fori_loop(0, size, one, 0, unroll=4)

    def transform(size, out, begin, scale):
        group = 8
        rows_half = 2 * size
        for g in range(rows_half // group):
            p, f = divmod(g * group, size)
            first = (p * size + f) * lines
            items = []
            for m in range(RADIX):
                re = weighted[pl.ds(first + 2 * m, group, stride=lines), :]
                im = weighted[pl.ds(first + 2 * m + 1, group, stride=lines), :]
                items.append((re, im))
            for k1, (re, im) in enumerate(butterflies(items)):
                if k1:
                    c, s = twid_ref[0, k1:k1 + 1, :], twid_ref[1, k1:k1 + 1, :]
                    re, im = re * c - im * s, re * s + im * c
                place = k1 * rows_half + g * group
                sections[place:place + group, :LANES] = re
                sections[place:place + group, LANES:] = im
        both = sections[0:RADIX * rows_half, :]
        high = both.astype(jnp.bfloat16)
        low = (both - high.astype(jnp.float32)).astype(jnp.bfloat16)
        dot = functools.partial(jnp.dot, preferred_element_type=jnp.float32)
        spec = dot(high, table_ref[0]) + (dot(high, table_ref[1]) + dot(low, table_ref[0]))
        spec = spec * spec
        both_pols = (spec[:, :LANES] + spec[:, LANES:]).reshape(RADIX, 2, size, LANES)
        energy = both_pols[:, 0] + both_pols[:, 1]
        chunk = lax.broadcasted_iota(jnp.int32, (size, LANES), 1) // RADIX
        for h in range(2):
            parts = [energy[8 * h + i] for i in range(8)]
            for bit in (4, 2, 1):
                kept = (chunk & bit) == 0
                for i in range(8):
                    if i & bit == 0:
                        low_part, high_part = parts[i], parts[i | bit]
                        parts[i] = jnp.where(kept, low_part, pltpu.roll(high_part, bit * RADIX, 1))
                        parts[i | bit] = jnp.where(kept, pltpu.roll(low_part, LANES - bit * RADIX, 1), high_part)
            for b in range(blocks):
                out[b, pl.ds(begin, size), h * LANES:(h + 1) * LANES] = parts[b] * (usable[h][b:b + 1] * scale)

    fir(EDGE, frames // 2)
    transform(frames // 2, spread_out, EDGE, 1.0)
    close_round(0)
    open_round(1)

    for b in range(NCHAN // LANES):
        block = delay_ref[:, b * LANES:(b + 1) * LANES].astype(jnp.float32)
        late_delay[b * LANES:(b + 1) * LANES, :] = jnp.concatenate([block, block], axis=0).T.astype(jnp.bfloat16)
    lane = lax.broadcasted_iota(jnp.int32, (16, LANES), 1)
    second = jnp.where(lane < trials, 0.0, float(HALF))
    at_once = 10

    def tally(g, carry):
        base = second + (g * at_once).astype(jnp.float32)
        levels = [(base + float(i)).astype(jnp.bfloat16) for i in range(at_once)]

        def some(k, sums):
            seen = late_delay[pl.ds(pl.multiple_of(k * 16, 16), 16), :]
            one = jnp.ones_like(seen)
            zero = jnp.zeros_like(seen)
            return tuple(t + jnp.where(seen >= level, one, zero) for t, level in zip(sums, levels))

        sums = lax.fori_loop(
            0, NCHAN // 16, some, tuple(jnp.zeros((16, LANES), jnp.bfloat16) for _ in range(at_once)), unroll=4
        )
        for i in range(at_once):
            counts[pl.ds(g * at_once + i, 1), :] = jnp.sum(sums[i].astype(jnp.float32), axis=0, keepdims=True)
        return carry

    lax.fori_loop(0, steps // at_once, tally, 0)
    close_round(1)
    open_round(2)
    order = lax.broadcasted_iota(jnp.int32, (wide, LANES), 0)
    order = ((order & (RADIX - 1)) * RADIX + order // RADIX).astype(jnp.float32).astype(jnp.bfloat16)

    def choose(i, carry):
        for side in range(2):
            total = counts[pl.ds(2 * i + side, 1), :].astype(jnp.int32)
            within = jnp.broadcast_to((total & (wide - 1)).astype(jnp.float32), (16, LANES)).astype(jnp.bfloat16)
            for g in range(wide // 16):
                mark = order[16 * g:16 * g + 16] < within
                picks[i, 16 * g:16 * g + 16, side * LANES:(side + 1) * LANES] = jnp.where(
                    mark, jnp.ones_like(within), jnp.zeros_like(within))
        return carry

    lax.fori_loop(0, steps // 2, choose, 0)
    acc[...] = jnp.zeros_like(acc)

    def dedisperse(source, size, offset):
        values = jnp.concatenate([source[b] for b in range(blocks)], axis=0).astype(jnp.bfloat16)
        dot = functools.partial(jnp.dot, preferred_element_type=jnp.float32)
        sums = dot(values, jnp.ones((wide, LANES), jnp.bfloat16))
        column = lax.broadcasted_iota(jnp.int32, (size, LANES), 1)
        prefix = jnp.zeros((size, LANES), jnp.float32)
        for b in range(blocks):
            prefix = prefix + jnp.where(column > b, sums[b * size:(b + 1) * size], 0.0)
        last = None
        for i in range(steps // 2):
            found = dot(values, picks[i])
            for side in range(2):
                j = 2 * i + side
                which = jnp.broadcast_to(counts[j:j + 1, :].astype(jnp.int32) // wide, (size, LANES))
                inner = jnp.zeros((size, LANES), jnp.float32)
                for b in range(blocks):
                    inner = jnp.where(which == b, found[b * size:(b + 1) * size, side * LANES:(side + 1) * LANES], inner)
                now = inner + jnp.take_along_axis(prefix, which, axis=1, mode="promise_in_bounds")
                if j:
                    change = last - now
                    if j - 1 == HALF:
                        change = jnp.where(column < trials, 0.0, change)
                    a, m = divmod(j - 1, 8)
                    place = HALF + EDGE + offset - 8 * a
                    acc[m, place:place + size] += change
                last = now

    @pl.when(me == 0)
    def _():
        for p in range(2):
            ext[p, 0:own] = jnp.zeros((own, lines, LANES), jnp.float32)
        fir(-EDGE, EDGE)
        transform(EDGE, early, 0, 1.0)
        dedisperse(early, EDGE, -EDGE)

    for i in range(2):
        from_before = lax.rem(me + i, 2) == 1
        begin = pl.multiple_of(jnp.where(from_before, 0, frames - EDGE), EDGE)

        @pl.when(from_before & (me > 0))
        def _():
            forward().wait_recv()
            for p in range(2):
                ext[p, EDGE:own] = before[p].astype(jnp.float32)

        @pl.when(jnp.logical_not(from_before) & (me < count - 1))
        def _():
            backward().wait_recv()
            for p in range(2):
                ext[p, own + frames:own + frames + EDGE] = after[p].astype(jnp.float32)

        @pl.when(jnp.logical_not(from_before) & (me == count - 1))
        def _():
            for p in range(2):
                ext[p, own + frames:own + frames + EDGE] = jnp.zeros((EDGE, lines, LANES), jnp.float32)

        fir(begin, EDGE)
        ended = jnp.logical_not(from_before) & (me == count - 1)
        transform(EDGE, spread_out, begin, jnp.where(ended, 0.0, 1.0))

    dedisperse(spread_out, frames, 0)
    height = HALF + frames + EDGE
    total = acc[0, 0:height]
    for m in range(1, 8):
        total = total + acc[m, m:m + height]
    side = lax.broadcasted_iota(jnp.int32, (8, LANES), 1) < trials
    empty = jnp.zeros((8, LANES), jnp.float32)

    def joined(r):
        first = total[r - HALF:r - HALF + 8] if HALF <= r < HALF + height else empty
        other = total[r:r + 8] if r < height else empty
        mixed = jnp.where(side, first, other)
        return mixed + pltpu.roll(mixed, trials, 1)

    half = frames // 2
    for q in range(reach + 1):
        for r in range(0, half, 8):
            top = joined(q * frames + r)
            low = joined(q * frames + half + r)
            part[q * half + r:q * half + r + 8, :] = jnp.where(side, top, low)
    rise = (reach + 1) * frames
    part[(reach + 1) * half:(reach + 1) * half + EDGE, :] = jnp.where(side, joined(rise), 0.0)

    def near(k):
        return pltpu.make_async_remote_copy(
            src_ref=part.at[pl.ds((reach - k) * half, half)], dst_ref=landed.at[k - 1],
            send_sem=near_send.at[k - 1], recv_sem=near_recv.at[k - 1],
            device_id={"tm": me - k}, device_id_type=MESH,
        )

    def up():
        return pltpu.make_async_remote_copy(
            src_ref=part.at[pl.ds((reach + 1) * half, EDGE)], dst_ref=risen,
            send_sem=near_send.at[reach], recv_sem=near_recv.at[reach],
            device_id={"tm": me + 1}, device_id_type=MESH,
        )

    for k in range(reach, 0, -1):
        @pl.when(me >= k)
        def _():
            near(k).start()

    @pl.when(me < count - 1)
    def _():
        up().start()

    for i in range(2, len(rounds)):
        close_round(i)
        open_round(i + 1)

    @pl.when(me == 0)
    def _():
        risen[...] = jnp.zeros_like(risen)

    @pl.when(me > 0)
    def _():
        up().wait_recv()

    for k in range(1, reach + 1):
        @pl.when(me + k >= count)
        def _():
            landed[k - 1] = jnp.zeros((half, LANES), jnp.float32)

        @pl.when(me + k < count)
        def _():
            near(k).wait_recv()

    series = part[reach * half:(reach + 1) * half, :]
    for k in range(1, reach + 1):
        series = series + landed[k - 1]
    series = series + jnp.concatenate([risen[...], jnp.zeros((half - EDGE, LANES), jnp.float32)], axis=0)
    lane = lax.broadcasted_iota(jnp.int32, (1, LANES), 1)

    def fold(value, op):
        return op(value, pltpu.roll(value, trials, 1))

    def low_half(value):
        return jnp.where(lane < trials, value, pltpu.roll(value, trials, 1))

    def high_half(value):
        return jnp.where(lane < trials, pltpu.roll(value, trials, 1), value)

    mean = fold(jnp.sum(series, axis=0, keepdims=True), jnp.add) * (1.0 / frames)
    away = series - mean
    spread = fold(jnp.sum(away * away, axis=0, keepdims=True), jnp.add)
    peak = fold(jnp.max(series, axis=0, keepdims=True), jnp.maximum)
    mine[...] = jnp.concatenate([jnp.where(lane < trials, mean, spread), peak], axis=0)

    def far(k):
        return pltpu.make_async_remote_copy(
            src_ref=mine, dst_ref=gathered.at[k - 1],
            send_sem=far_send.at[k - 1], recv_sem=far_recv.at[k - 1],
            device_id={"tm": lax.rem(me + k, count)}, device_id_type=MESH,
        )

    for k in range(1, count):
        far(k).start()
    live = jnp.maximum(jnp.sum(mask_ref[...].astype(jnp.float32)), 1.0)
    for k in range(1, count):
        far(k).wait_recv()
    sums = gathered[:, 0, :]
    tops = gathered[:, 1, :]
    average = (mean + low_half(jnp.sum(sums, axis=0, keepdims=True))) * (1.0 / count)
    offset = sums - average
    squares = spread + high_half(jnp.sum(sums, axis=0, keepdims=True))
    between = (mean - average) * (mean - average) + low_half(jnp.sum(offset * offset, axis=0, keepdims=True))
    variance = (squares + frames * between) * (1.0 / (frames * count))
    top = jnp.maximum(peak, jnp.max(tops, axis=0, keepdims=True))
    deviation = jnp.sqrt(variance + 1e-05)
    z = (series - average) / deviation
    z_ref[0:half, :] = z[:, :trials]
    z_ref[half:frames, :] = pltpu.roll(z, trials, 1)[:, :trials]
    stats_ref[...] = jnp.concatenate(
        [average / live, deviation / live, (top - average) / deviation], axis=0
    )[:, :trials]

    @pl.when(me < count - 1)
    def _():
        forward().wait_send()
        up().wait_send()

    @pl.when(me > 0)
    def _():
        backward().wait_send()

    for k in range(1, reach + 1):
        @pl.when(me >= k)
        def _():
            near(k).wait_send()
    for k in range(1, count):
        far(k).wait_send()


def finish_kernel(z_ref, stats_ref, z_out, stats_out, sem):
    first = pltpu.make_async_copy(z_ref, z_out, sem.at[0])
    second = pltpu.make_async_copy(stats_ref, stats_out, sem.at[1])
    first.start()
    second.start()
    first.wait()
    second.wait()


def per_device(voltage, delays, chan_mask):
    frames = voltage.shape[2] // NCHAN
    trials = delays.shape[0]
    count = lax.axis_size("tm")
    lines = 2 * RADIX
    half = frames // 2
    blocks = LANES // RADIX
    wide = NCHAN // blocks
    reach = MAXD // frames
    steps = HALF + 2
    past = TAPS - 1
    vmem = pl.BlockSpec(memory_space=pltpu.VMEM)
    hbm = pl.BlockSpec(memory_space=pltpu.HBM)
    framed = voltage.reshape(2, 2, frames * RADIX, LANES).transpose(0, 2, 1, 3).reshape(2, frames, lines, LANES)
    operands = (framed, jnp.asarray(prototype()), jnp.asarray(twiddles()), jnp.asarray(transform_table()), delays,
                chan_mask.reshape(RADIX, LANES))
    dma = pltpu.SemaphoreType.DMA
    outputs = (
        jax.ShapeDtypeStruct((frames, trials), jnp.float32),
        jax.ShapeDtypeStruct((3, trials), jnp.float32),
    )
    results = pl.pallas_call(
        functools.partial(beam_kernel, count, frames, trials),
        out_shape=outputs,
        in_specs=[hbm] * 6,
        out_specs=(vmem,) * 2,
        scratch_shapes=[
            pltpu.VMEM((2, frames, lines, LANES), jnp.bfloat16),
            pltpu.VMEM((TAPS, lines, LANES), jnp.float32),
            pltpu.VMEM((2, RADIX, LANES), jnp.float32),
            pltpu.VMEM((2, 2 * LANES, 2 * LANES), jnp.bfloat16),
            pltpu.VMEM((trials, NCHAN), jnp.int32),
            pltpu.VMEM((RADIX, LANES), jnp.int32),
            pltpu.VMEM((2, past - EDGE, lines, LANES), jnp.bfloat16),
            pltpu.VMEM((2, EDGE, lines, LANES), jnp.bfloat16),
            pltpu.VMEM((2, frames + past + EDGE, lines, LANES), jnp.float32),
            pltpu.VMEM((frames * lines, LANES), jnp.float32),
            pltpu.VMEM((RADIX * frames, 2 * LANES), jnp.float32),
            pltpu.VMEM((blocks, frames, 2 * LANES), jnp.float32),
            pltpu.VMEM((blocks, EDGE, 2 * LANES), jnp.float32),
            pltpu.VMEM((NCHAN, LANES), jnp.bfloat16),
            pltpu.VMEM((steps + 6, LANES), jnp.float32),
            pltpu.VMEM((steps // 2, wide, 2 * LANES), jnp.bfloat16),
            pltpu.VMEM((8, HALF + frames + 2 * EDGE, LANES), jnp.float32),
            pltpu.VMEM(((reach + 1) * half + EDGE, LANES), jnp.float32),
            pltpu.VMEM((reach, half, LANES), jnp.float32),
            pltpu.VMEM((EDGE, LANES), jnp.float32),
            pltpu.VMEM((2, LANES), jnp.float32),
            pltpu.VMEM((count - 1, 2, LANES), jnp.float32),
            dma((6,)),
            dma((2,)),
            dma((2,)),
            dma((reach + 1,)),
            dma((reach + 1,)),
            dma((count - 1,)),
            dma((count - 1,)),
            pltpu.SemaphoreType.REGULAR((8,)),
        ],
        compiler_params=pltpu.CompilerParams(collective_id=1, vmem_limit_bytes=GRANT, has_side_effects=True),
        name="beam",
    )(*[pltpu.with_memory_space_constraint(v, pltpu.HBM) for v in operands])
    zscore, trial_stats = pl.pallas_call(
        finish_kernel,
        out_shape=outputs,
        in_specs=[vmem] * 2,
        out_specs=(hbm,) * 2,
        scratch_shapes=[dma((2,))],
        compiler_params=pltpu.CompilerParams(vmem_limit_bytes=GRANT),
        name="finish",
    )(*results)
    return (zscore.T, trial_stats)


def solution(mesh):
    in_specs = (P(None, None, ("beam", "tm")), P(), P("beam"))
    out_specs = (P(None, ("beam", "tm")), P(None, "beam"))
    return jax.shard_map(
        per_device, mesh=mesh, in_specs=in_specs, out_specs=out_specs, check_vma=False
    )
```

time: 23.7 us -> 27.9 us (1.18)
  Pallas kernels: 22.9 us -> 27.1 us
    pallas_call x4 -> x2, Pallas kernels: 22.9 us -> 27.1 us  [the longest x1 26.5 us: per_device(): pl.pallas_call(functools.partial(beam_kernel, count, frames, trials), out...]
where the time goes in v2:
time: 27.9 us; the launch traced here: 27.8 us
  Pallas kernels  27.1 us (97%)
  between operations  0.64 us (2%)
    pallas_call x1, Pallas kernels, per_device(): pl.pallas_call(functools.partial(beam_kernel, count, frames, trials), out...  26.5 us
    pallas_call x1, Pallas kernels, per_device(): pl.pallas_call(finish_kernel, out_shape=outputs, in_specs=[vmem] * 2, out...  0.63 us

profile of v2, /device:TPU:0, one launch (start us, length us, event | category | flops | bytes accessed | tf_op | source)
XLA Modules:
  0.0 27.8 jit_solution(18219551178755805489)
XLA Ops:
  0.6 26.5 %beam.1 = (f32[32,64]{1,0:T(8,128)S(1)}, f32[3,64]{1,0:T(4,128)S(1)}) custom-call(bf16[2,32,32,128]{3,2,1,0:T(8,128)(2,1)} %bitcast.7, f32[16,32,128]{2,1,0:T(8,128)} %constant.6.clone.taps_hbm, f32[2,16,128]{2,1,0:T(8,128)} %constant.7.clone.twid_hbm, bf16[2,256,256]{2,1,0:T(8,128)(2,1)} %constant.8.clone.table_hbm, s32[64,2048]{1,0:T(8,128)} %delay_hbm.1, ...), custom_call_target="tpu_custom_call" | custom-call | tf_op jit(solution)/shard_map/beam/pallas_call | solution.py:499
  27.1 0.6 %finish.1 = (f32[32,64]{1,0:T(8,128)}, f32[3,64]{1,0:T(4,128)}) custom-call(f32[32,64]{1,0:T(8,128)S(1)} %get-tuple-element.6.z_ref, f32[3,64]{1,0:T(4,128)S(1)} %get-tuple-element.7.stats_ref), custom_call_target="tpu_custom_call" | custom-call | tf_op jit(solution)/shard_map/finish/pallas_call | solution.py:539

commit v3 on v2

--- a/solution.py
+++ b/solution.py
@@ -16,6 +16,7 @@
 MAXD = 96
 EDGE = 8
 HALF = MAXD // 2
+PITCH = 40
 GRANT = 32 * 1024 * 1024
 MESH = pl.DeviceIdType.MESH
 
@@ -83,7 +84,7 @@
 
 def beam_kernel(count, frames, trials, volt_hbm, taps_hbm, twid_hbm, table_hbm, delay_hbm, mask_hbm, z_ref, stats_ref,
                 volt_ref, taps_ref, twid_ref, table_ref, delay_ref, mask_ref, before, after, ext, weighted, sections,
-                spread_out, early, late_delay, counts, picks, acc, part, landed, risen, mine, gathered,
+                spread_out, early, blockno, within, picks, acc, part, landed, risen, mine, gathered,
                 load_sem, halo_send, halo_recv, near_send, near_recv, far_send, far_recv, know):
     me = lax.axis_index("tm")
     past = TAPS - 1
@@ -110,7 +111,7 @@
     close = [k for d in range(1, reach + 1) for k in (-d, d)]
     for k in close:
         tell(barrier, k)
-    pairs = ((volt_hbm, volt_ref), (taps_hbm, taps_ref), (delay_hbm, delay_ref), (twid_hbm, twid_ref),
+    pairs = ((volt_hbm, volt_ref), (taps_hbm, taps_ref.at[:, pl.ds(0, lines)]), (delay_hbm, delay_ref), (twid_hbm, twid_ref),
              (table_hbm, table_ref), (mask_hbm, mask_ref))
     loads = [pltpu.make_async_copy(a, b, load_sem.at[i]) for i, (a, b) in enumerate(pairs)]
     for load in loads:
@@ -156,7 +157,7 @@
 
     open_round(0)
     for p in range(2):
-        ext[p, own:own + frames] = volt_ref[p].astype(jnp.float32)
+        ext[p, own:own + frames, 0:lines] = volt_ref[p].astype(jnp.float32)
     for load in loads[1:]:
         load.wait()
 
@@ -165,7 +166,7 @@
     odd = mask_ref[pl.ds(1, blocks, stride=2), :]
     usable = []
     for h in range(2):
-        place = (row & 7) * RADIX + 8 * h + row // RADIX
+        place = (row & 7) * RADIX + 8 * h + (row >> 4)
         low = jnp.take_along_axis(even, place, axis=1, mode="promise_in_bounds")
         high = jnp.take_along_axis(odd, place, axis=1, mode="promise_in_bounds")
         usable.append(jnp.where((row & 8) == 0, low, high).astype(jnp.float32))
@@ -175,27 +176,32 @@
             rows = pl.ds(8 * part_index, 8)
             taps = [taps_ref[j, rows, :] for j in range(TAPS)]
 
-            def one(f, carry):
+            def some(g, carry):
                 for p in range(2):
-                    terms = [taps[j] * ext[p, begin + EDGE + f + j, rows, :] for j in range(TAPS)]
-                    while len(terms) > 1:
-                        terms = [a + b for a, b in zip(terms[0::2], terms[1::2])]
-                    start = pl.multiple_of((p * size + f) * lines, 8) + 8 * part_index
-                    weighted[pl.ds(start, 8), :] = terms[0]
+                    sums = [None] * 4
+                    for i in range(TAPS + 3):
+                        sample = ext[p, begin + EDGE + 4 * g + i, rows, :]
+                        for f in range(4):
+                            if 0 <= i - f < TAPS:
+                                term = taps[i - f] * sample
+                                sums[f] = term if sums[f] is None else sums[f] + term
+                    for f in range(4):
+                        start = pl.multiple_of((p * size + 4 * g + f) * PITCH, 8) + 8 * part_index
+                        weighted[pl.ds(start, 8), :] = sums[f]
                 return carry
 
-            lax.fori_loop(0, size, one, 0, unroll=4)
+            lax.fori_loop(0, size // 4, some, 0)
 
     def transform(size, out, begin, scale):
         group = 8
         rows_half = 2 * size
         for g in range(rows_half // group):
             p, f = divmod(g * group, size)
-            first = (p * size + f) * lines
+            first = (p * size + f) * PITCH
             items = []
             for m in range(RADIX):
-                re = weighted[pl.ds(first + 2 * m, group, stride=lines), :]
-                im = weighted[pl.ds(first + 2 * m + 1, group, stride=lines), :]
+                re = weighted[pl.ds(first + 2 * m, group, stride=PITCH), :]
+                im = weighted[pl.ds(first + 2 * m + 1, group, stride=PITCH), :]
                 items.append((re, im))
             for k1, (re, im) in enumerate(butterflies(items)):
                 if k1:
@@ -212,7 +218,7 @@
         spec = spec * spec
         both_pols = (spec[:, :LANES] + spec[:, LANES:]).reshape(RADIX, 2, size, LANES)
         energy = both_pols[:, 0] + both_pols[:, 1]
-        chunk = lax.broadcasted_iota(jnp.int32, (size, LANES), 1) // RADIX
+        chunk = lax.broadcasted_iota(jnp.int32, (size, LANES), 1) >> 4
         for h in range(2):
             parts = [energy[8 * h + i] for i in range(8)]
             for bit in (4, 2, 1):
@@ -230,44 +236,48 @@
     close_round(0)
     open_round(1)
 
-    for b in range(NCHAN // LANES):
-        block = delay_ref[:, b * LANES:(b + 1) * LANES].astype(jnp.float32)
-        late_delay[b * LANES:(b + 1) * LANES, :] = jnp.concatenate([block, block], axis=0).T.astype(jnp.bfloat16)
-    lane = lax.broadcasted_iota(jnp.int32, (16, LANES), 1)
-    second = jnp.where(lane < trials, 0.0, float(HALF))
-    at_once = 10
-
-    def tally(g, carry):
-        base = second + (g * at_once).astype(jnp.float32)
-        levels = [(base + float(i)).astype(jnp.bfloat16) for i in range(at_once)]
-
-        def some(k, sums):
-            seen = late_delay[pl.ds(pl.multiple_of(k * 16, 16), 16), :]
-            one = jnp.ones_like(seen)
-            zero = jnp.zeros_like(seen)
-            return tuple(t + jnp.where(seen >= level, one, zero) for t, level in zip(sums, levels))
-
-        sums = lax.fori_loop(
-            0, NCHAN // 16, some, tuple(jnp.zeros((16, LANES), jnp.bfloat16) for _ in range(at_once)), unroll=4
-        )
-        for i in range(at_once):
-            counts[pl.ds(g * at_once + i, 1), :] = jnp.sum(sums[i].astype(jnp.float32), axis=0, keepdims=True)
-        return carry
-
-    lax.fori_loop(0, steps // at_once, tally, 0)
+    level = lax.broadcasted_iota(jnp.int32, (trials, LANES), 1)
+
+    def look(table, place):
+        return jnp.take_along_axis(table, place, axis=1, mode="promise_in_bounds")
+
+    tables = NCHAN // LANES
+    seldom = jnp.zeros((trials, LANES), jnp.int32)
+    each = (level & (LANES // tables - 1)) * tables + (tables - 1)
+    for b in range(tables):
+        seen = look(delay_ref[:, b * LANES:(b + 1) * LANES], each)
+        seldom = jnp.where((level >> 3) == b, seen, seldom)
+    coarse = jnp.zeros((trials, LANES), jnp.int32)
+    for step in (64, 32, 16, 8, 4, 2, 1):
+        seen = look(seldom, coarse + (step - 1))
+        coarse = jnp.where(seen >= level, coarse + step, coarse)
+    which = coarse >> 3
+    start = (coarse & 7) * tables
+    fine = jnp.zeros((trials, LANES), jnp.int32)
+    for step in (8, 4, 2, 1):
+        place = start + fine + (step - 1)
+        seen = jnp.full((trials, LANES), -1, jnp.int32)
+        for b in range(tables):
+            seen = jnp.where(which == b, look(delay_ref[:, b * LANES:(b + 1) * LANES], place), seen)
+        fine = jnp.where(seen >= level, fine + step, fine)
+    total = jnp.where(level == 0, NCHAN, coarse * tables + fine).astype(jnp.float32)
+    turned = jnp.concatenate([total, jnp.zeros((LANES - trials, LANES), jnp.float32)], axis=0).T
+    rows_kept = blockno.shape[0]
+    near_side = lax.broadcasted_iota(jnp.int32, (rows_kept, LANES), 1) < trials
+    total = jnp.where(
+        near_side, turned[0:rows_kept], pltpu.roll(turned[HALF:HALF + rows_kept], trials, 1)
+    ).astype(jnp.int32)
+    blockno[...] = total >> 8
+    within[...] = (total & (wide - 1)).astype(jnp.float32)
     close_round(1)
     open_round(2)
     order = lax.broadcasted_iota(jnp.int32, (wide, LANES), 0)
-    order = ((order & (RADIX - 1)) * RADIX + order // RADIX).astype(jnp.float32).astype(jnp.bfloat16)
+    order = ((order & (RADIX - 1)) * RADIX + (order >> 4)).astype(jnp.float32)
 
     def choose(i, carry):
         for side in range(2):
-            total = counts[pl.ds(2 * i + side, 1), :].astype(jnp.int32)
-            within = jnp.broadcast_to((total & (wide - 1)).astype(jnp.float32), (16, LANES)).astype(jnp.bfloat16)
-            for g in range(wide // 16):
-                mark = order[16 * g:16 * g + 16] < within
-                picks[i, 16 * g:16 * g + 16, side * LANES:(side + 1) * LANES] = jnp.where(
-                    mark, jnp.ones_like(within), jnp.zeros_like(within))
+            end = jnp.broadcast_to(within[pl.ds(2 * i + side, 1), :], (wide, LANES))
+            picks[i, :, side * LANES:(side + 1) * LANES] = jnp.where(order < end, 1.0, 0.0).astype(jnp.bfloat16)
         return carry
 
     lax.fori_loop(0, steps // 2, choose, 0)
@@ -286,7 +296,7 @@
             found = dot(values, picks[i])
             for side in range(2):
                 j = 2 * i + side
-                which = jnp.broadcast_to(counts[j:j + 1, :].astype(jnp.int32) // wide, (size, LANES))
+                which = jnp.broadcast_to(blockno[j:j + 1, :], (size, LANES))
                 inner = jnp.zeros((size, LANES), jnp.float32)
                 for b in range(blocks):
                     inner = jnp.where(which == b, found[b * size:(b + 1) * size, side * LANES:(side + 1) * LANES], inner)
@@ -303,7 +313,7 @@
     @pl.when(me == 0)
     def _():
         for p in range(2):
-            ext[p, 0:own] = jnp.zeros((own, lines, LANES), jnp.float32)
+            ext[p, 0:own, 0:lines] = jnp.zeros((own, lines, LANES), jnp.float32)
         fir(-EDGE, EDGE)
         transform(EDGE, early, 0, 1.0)
         dedisperse(early, EDGE, -EDGE)
@@ -316,18 +326,18 @@
         def _():
             forward().wait_recv()
             for p in range(2):
-                ext[p, EDGE:own] = before[p].astype(jnp.float32)
+                ext[p, EDGE:own, 0:lines] = before[p].astype(jnp.float32)
 
         @pl.when(jnp.logical_not(from_before) & (me < count - 1))
         def _():
             backward().wait_recv()
             for p in range(2):
-                ext[p, own + frames:own + frames + EDGE] = after[p].astype(jnp.float32)
+                ext[p, own + frames:own + frames + EDGE, 0:lines] = after[p].astype(jnp.float32)
 
         @pl.when(jnp.logical_not(from_before) & (me == count - 1))
         def _():
             for p in range(2):
-                ext[p, own + frames:own + frames + EDGE] = jnp.zeros((EDGE, lines, LANES), jnp.float32)
+                ext[p, own + frames:own + frames + EDGE, 0:lines] = jnp.zeros((EDGE, lines, LANES), jnp.float32)
 
         fir(begin, EDGE)
         ended = jnp.logical_not(from_before) & (me == count - 1)
@@ -503,19 +513,19 @@
         out_specs=(vmem,) * 2,
         scratch_shapes=[
             pltpu.VMEM((2, frames, lines, LANES), jnp.bfloat16),
-            pltpu.VMEM((TAPS, lines, LANES), jnp.float32),
+            pltpu.VMEM((TAPS, PITCH, LANES), jnp.float32),
             pltpu.VMEM((2, RADIX, LANES), jnp.float32),
             pltpu.VMEM((2, 2 * LANES, 2 * LANES), jnp.bfloat16),
             pltpu.VMEM((trials, NCHAN), jnp.int32),
             pltpu.VMEM((RADIX, LANES), jnp.int32),
             pltpu.VMEM((2, past - EDGE, lines, LANES), jnp.bfloat16),
             pltpu.VMEM((2, EDGE, lines, LANES), jnp.bfloat16),
-            pltpu.VMEM((2, frames + past + EDGE, lines, LANES), jnp.float32),
-            pltpu.VMEM((frames * lines, LANES), jnp.float32),
+            pltpu.VMEM((2, frames + past + EDGE, PITCH, LANES), jnp.float32),
+            pltpu.VMEM((frames * PITCH, LANES), jnp.float32),
             pltpu.VMEM((RADIX * frames, 2 * LANES), jnp.float32),
             pltpu.VMEM((blocks, frames, 2 * LANES), jnp.float32),
             pltpu.VMEM((blocks, EDGE, 2 * LANES), jnp.float32),
-            pltpu.VMEM((NCHAN, LANES), jnp.bfloat16),
+            pltpu.VMEM((steps + 6, LANES), jnp.int32),
             pltpu.VMEM((steps + 6, LANES), jnp.float32),
             pltpu.VMEM((steps // 2, wide, 2 * LANES), jnp.bfloat16),
             pltpu.VMEM((8, HALF + frames + 2 * EDGE, LANES), jnp.float32),

time: 27.9 us -> 21.9 us (0.78)
  Pallas kernels: 27.1 us -> 21.1 us
    pallas_call x1, Pallas kernels: 26.5 us -> 20.5 us  [per_device(): pl.pallas_call(functools.partial(beam_kernel, count, frames, trials), out...]
where the time goes in v3:
time: 21.9 us; the launch traced here: 21.8 us
  Pallas kernels  21.1 us (96%)
  between operations  0.64 us (3%)
    pallas_call x1, Pallas kernels, per_device(): pl.pallas_call(functools.partial(beam_kernel, count, frames, trials), out...  20.5 us
    pallas_call x1, Pallas kernels, per_device(): pl.pallas_call(finish_kernel, out_shape=outputs, in_specs=[vmem] * 2, out...  0.63 us

profile of v3, /device:TPU:0, one launch (start us, length us, event | category | flops | bytes accessed | tf_op | source)
XLA Modules:
  0.0 21.8 jit_solution(1343529636122503730)
XLA Ops:
  0.6 20.5 %beam.1 = (f32[32,64]{1,0:T(8,128)S(1)}, f32[3,64]{1,0:T(4,128)S(1)}) custom-call(bf16[2,32,32,128]{3,2,1,0:T(8,128)(2,1)} %bitcast.7, f32[16,32,128]{2,1,0:T(8,128)} %constant.6.clone.taps_hbm, f32[2,16,128]{2,1,0:T(8,128)} %constant.7.clone.twid_hbm, bf16[2,256,256]{2,1,0:T(8,128)(2,1)} %constant.8.clone.table_hbm, s32[64,2048]{1,0:T(8,128)} %delay_hbm.1, ...), custom_call_target="tpu_custom_call" | custom-call | tf_op jit(solution)/shard_map/beam/pallas_call | solution.py:509
  21.1 0.6 %finish.1 = (f32[32,64]{1,0:T(8,128)}, f32[3,64]{1,0:T(4,128)}) custom-call(f32[32,64]{1,0:T(8,128)S(1)} %get-tuple-element.6.z_ref, f32[3,64]{1,0:T(4,128)S(1)} %get-tuple-element.7.stats_ref), custom_call_target="tpu_custom_call" | custom-call | tf_op jit(solution)/shard_map/finish/pallas_call | solution.py:549

commit v4 on v3

--- a/solution.py
+++ b/solution.py
@@ -84,7 +84,7 @@
 
 def beam_kernel(count, frames, trials, volt_hbm, taps_hbm, twid_hbm, table_hbm, delay_hbm, mask_hbm, z_ref, stats_ref,
                 volt_ref, taps_ref, twid_ref, table_ref, delay_ref, mask_ref, before, after, ext, weighted, sections,
-                spread_out, early, blockno, within, picks, acc, part, landed, risen, mine, gathered,
+                spread_out, early, blockno, within, acc, part, landed, risen, mine, gathered,
                 load_sem, halo_send, halo_recv, near_send, near_recv, far_send, far_recv, know):
     me = lax.axis_index("tm")
     past = TAPS - 1
@@ -130,6 +130,8 @@
         )
 
     loads[0].wait()
+    for p in range(2):
+        ext[p, own:own + frames, 0:lines] = volt_ref[p].astype(jnp.float32)
     wait_some(barrier, number(close))
 
     @pl.when(me < count - 1)
@@ -156,8 +158,6 @@
             wait_some(know.at[i], number((-rounds[i], rounds[i])))
 
     open_round(0)
-    for p in range(2):
-        ext[p, own:own + frames, 0:lines] = volt_ref[p].astype(jnp.float32)
     for load in loads[1:]:
         load.wait()
 
@@ -236,31 +236,40 @@
     close_round(0)
     open_round(1)
 
-    level = lax.broadcasted_iota(jnp.int32, (trials, LANES), 1)
+    level = lax.broadcasted_iota(jnp.int32, (8, LANES), 1)
 
     def look(table, place):
         return jnp.take_along_axis(table, place, axis=1, mode="promise_in_bounds")
 
     tables = NCHAN // LANES
-    seldom = jnp.zeros((trials, LANES), jnp.int32)
+    groups = range(trials // 8)
     each = (level & (LANES // tables - 1)) * tables + (tables - 1)
-    for b in range(tables):
-        seen = look(delay_ref[:, b * LANES:(b + 1) * LANES], each)
-        seldom = jnp.where((level >> 3) == b, seen, seldom)
-    coarse = jnp.zeros((trials, LANES), jnp.int32)
+
+    def table(g, b):
+        return delay_ref[8 * g:8 * g + 8, b * LANES:(b + 1) * LANES]
+
+    seldom = []
+    for g in groups:
+        kept = jnp.zeros((8, LANES), jnp.int32)
+        for b in range(tables):
+            kept = jnp.where((level >> 3) == b, look(table(g, b), each), kept)
+        seldom.append(kept)
+    coarse = [jnp.zeros((8, LANES), jnp.int32) for g in groups]
     for step in (64, 32, 16, 8, 4, 2, 1):
-        seen = look(seldom, coarse + (step - 1))
-        coarse = jnp.where(seen >= level, coarse + step, coarse)
-    which = coarse >> 3
-    start = (coarse & 7) * tables
-    fine = jnp.zeros((trials, LANES), jnp.int32)
+        for g in groups:
+            seen = look(seldom[g], coarse[g] + (step - 1))
+            coarse[g] = jnp.where(seen >= level, coarse[g] + step, coarse[g])
+    fine = [jnp.zeros((8, LANES), jnp.int32) for g in groups]
     for step in (8, 4, 2, 1):
-        place = start + fine + (step - 1)
-        seen = jnp.full((trials, LANES), -1, jnp.int32)
-        for b in range(tables):
-            seen = jnp.where(which == b, look(delay_ref[:, b * LANES:(b + 1) * LANES], place), seen)
-        fine = jnp.where(seen >= level, fine + step, fine)
-    total = jnp.where(level == 0, NCHAN, coarse * tables + fine).astype(jnp.float32)
+        for g in groups:
+            place = (coarse[g] & 7) * tables + fine[g] + (step - 1)
+            which = coarse[g] >> 3
+            seen = jnp.full((8, LANES), -1, jnp.int32)
+            for b in range(tables):
+                seen = jnp.where(which == b, look(table(g, b), place), seen)
+            fine[g] = jnp.where(seen >= level, fine[g] + step, fine[g])
+    total = jnp.concatenate(
+        [jnp.where(level == 0, NCHAN, coarse[g] * tables + fine[g]).astype(jnp.float32) for g in groups], axis=0)
     turned = jnp.concatenate([total, jnp.zeros((LANES - trials, LANES), jnp.float32)], axis=0).T
     rows_kept = blockno.shape[0]
     near_side = lax.broadcasted_iota(jnp.int32, (rows_kept, LANES), 1) < trials
@@ -274,13 +283,12 @@
     order = lax.broadcasted_iota(jnp.int32, (wide, LANES), 0)
     order = ((order & (RADIX - 1)) * RADIX + (order >> 4)).astype(jnp.float32)
 
-    def choose(i, carry):
-        for side in range(2):
-            end = jnp.broadcast_to(within[pl.ds(2 * i + side, 1), :], (wide, LANES))
-            picks[i, :, side * LANES:(side + 1) * LANES] = jnp.where(order < end, 1.0, 0.0).astype(jnp.bfloat16)
-        return carry
-
-    lax.fori_loop(0, steps // 2, choose, 0)
+    order = order.astype(jnp.bfloat16)
+
+    def pick(j):
+        end = jnp.broadcast_to(within[j:j + 1, :], (wide, LANES)).astype(jnp.bfloat16)
+        return jnp.minimum(jnp.maximum(end - order, jnp.zeros_like(end)), jnp.ones_like(end))
+
     acc[...] = jnp.zeros_like(acc)
 
     def dedisperse(source, size, offset):
@@ -293,7 +301,7 @@
             prefix = prefix + jnp.where(column > b, sums[b * size:(b + 1) * size], 0.0)
         last = None
         for i in range(steps // 2):
-            found = dot(values, picks[i])
+            found = dot(values, jnp.concatenate([pick(2 * i), pick(2 * i + 1)], axis=1))
             for side in range(2):
                 j = 2 * i + side
                 which = jnp.broadcast_to(blockno[j:j + 1, :], (size, LANES))
@@ -527,7 +535,6 @@
             pltpu.VMEM((blocks, EDGE, 2 * LANES), jnp.float32),
             pltpu.VMEM((steps + 6, LANES), jnp.int32),
             pltpu.VMEM((steps + 6, LANES), jnp.float32),
-            pltpu.VMEM((steps // 2, wide, 2 * LANES), jnp.bfloat16),
             pltpu.VMEM((8, HALF + frames + 2 * EDGE, LANES), jnp.float32),
             pltpu.VMEM(((reach + 1) * half + EDGE, LANES), jnp.float32),
             pltpu.VMEM((reach, half, LANES), jnp.float32),

time: 21.9 us -> 20.2 us (0.922)
  Pallas kernels: 21.1 us -> 19.4 us
    pallas_call x1, Pallas kernels: 20.5 us -> 18.8 us  [per_device(): pl.pallas_call(functools.partial(beam_kernel, count, frames, trials), out...]
where the time goes in v4:
time: 20.2 us; the launch traced here: 20.1 us
  Pallas kernels  19.4 us (96%)
  between operations  0.64 us (3%)
    pallas_call x1, Pallas kernels, per_device(): pl.pallas_call(functools.partial(beam_kernel, count, frames, trials), out...  18.8 us
    pallas_call x1, Pallas kernels, per_device(): pl.pallas_call(finish_kernel, out_shape=outputs, in_specs=[vmem] * 2, out...  0.63 us

profile of v4, /device:TPU:0, one launch (start us, length us, event | category | flops | bytes accessed | tf_op | source)
XLA Modules:
  0.0 20.1 jit_solution(15658068574433082008)
XLA Ops:
  0.6 18.8 %beam.1 = (f32[32,64]{1,0:T(8,128)S(1)}, f32[3,64]{1,0:T(4,128)S(1)}) custom-call(bf16[2,32,32,128]{3,2,1,0:T(8,128)(2,1)} %bitcast.7, f32[16,32,128]{2,1,0:T(8,128)} %constant.6.clone.taps_hbm, f32[2,16,128]{2,1,0:T(8,128)} %constant.7.clone.twid_hbm, bf16[2,256,256]{2,1,0:T(8,128)(2,1)} %constant.8.clone.table_hbm, s32[64,2048]{1,0:T(8,128)} %delay_hbm.1, ...), custom_call_target="tpu_custom_call" | custom-call | tf_op jit(solution)/shard_map/beam/pallas_call | solution.py:517
  19.4 0.6 %finish.1 = (f32[32,64]{1,0:T(8,128)}, f32[3,64]{1,0:T(4,128)}) custom-call(f32[32,64]{1,0:T(8,128)S(1)} %get-tuple-element.6.z_ref, f32[3,64]{1,0:T(4,128)S(1)} %get-tuple-element.7.stats_ref), custom_call_target="tpu_custom_call" | custom-call | tf_op jit(solution)/shard_map/finish/pallas_call | solution.py:556

commit v5 on v4

--- a/solution.py
+++ b/solution.py
@@ -84,8 +84,8 @@
 
 def beam_kernel(count, frames, trials, volt_hbm, taps_hbm, twid_hbm, table_hbm, delay_hbm, mask_hbm, z_ref, stats_ref,
                 volt_ref, taps_ref, twid_ref, table_ref, delay_ref, mask_ref, before, after, ext, weighted, sections,
-                spread_out, early, blockno, within, acc, part, landed, risen, mine, gathered,
-                load_sem, halo_send, halo_recv, near_send, near_recv, far_send, far_recv, know):
+                spread_out, early, tally, blockno, within, acc, part, landed, risen, mine, gathered,
+                load_sem, halo_send, halo_recv, near_send, near_recv, far_send, far_recv, swap_sem, know):
     me = lax.axis_index("tm")
     past = TAPS - 1
     lead = past - EDGE
@@ -95,6 +95,9 @@
     wide = NCHAN // blocks
     reach = MAXD // frames
     steps = HALF + 2
+    share = trials // 2
+    core = lax.rem(me, 2)
+    first = pl.multiple_of(core * share, share)
     barrier = pltpu.get_barrier_semaphore()
 
     def here(k):
@@ -108,10 +111,10 @@
     def number(distances):
         return sum(jnp.where(here(k), 1, 0) for k in distances)
 
-    close = [k for d in range(1, reach + 1) for k in (-d, d)]
+    close = (-1, 1)
     for k in close:
         tell(barrier, k)
-    pairs = ((volt_hbm, volt_ref), (taps_hbm, taps_ref.at[:, pl.ds(0, lines)]), (delay_hbm, delay_ref), (twid_hbm, twid_ref),
+    pairs = ((volt_hbm, volt_ref), (taps_hbm, taps_ref.at[:, pl.ds(0, lines)]), (delay_hbm.at[pl.ds(first, share)], delay_ref), (twid_hbm, twid_ref),
              (table_hbm, table_ref), (mask_hbm, mask_ref))
     loads = [pltpu.make_async_copy(a, b, load_sem.at[i]) for i, (a, b) in enumerate(pairs)]
     for load in loads:
@@ -134,7 +137,7 @@
         ext[p, own:own + frames, 0:lines] = volt_ref[p].astype(jnp.float32)
     wait_some(barrier, number(close))
 
-    @pl.when(me < count - 1)
+    @pl.when((core == 1) & (me < count - 1))
     def _():
         forward().start()
 
@@ -142,8 +145,12 @@
     def _():
         backward().start()
 
+    @pl.when((core == 0) & (me < count - 1))
+    def _():
+        forward().start()
+
     rounds = []
-    known = reach
+    known = 1
     while known < count - 1:
         rounds.append(known)
         known *= 2
@@ -231,18 +238,13 @@
             for b in range(blocks):
                 out[b, pl.ds(begin, size), h * LANES:(h + 1) * LANES] = parts[b] * (usable[h][b:b + 1] * scale)
 
-    fir(EDGE, frames // 2)
-    transform(frames // 2, spread_out, EDGE, 1.0)
-    close_round(0)
-    open_round(1)
-
     level = lax.broadcasted_iota(jnp.int32, (8, LANES), 1)
 
     def look(table, place):
         return jnp.take_along_axis(table, place, axis=1, mode="promise_in_bounds")
 
     tables = NCHAN // LANES
-    groups = range(trials // 8)
+    groups = range(share // 8)
     each = (level & (LANES // tables - 1)) * tables + (tables - 1)
 
     def table(g, b):
@@ -268,8 +270,27 @@
             for b in range(tables):
                 seen = jnp.where(which == b, look(table(g, b), place), seen)
             fine[g] = jnp.where(seen >= level, fine[g] + step, fine[g])
-    total = jnp.concatenate(
+    tally[pl.ds(first, share), :] = jnp.concatenate(
         [jnp.where(level == 0, NCHAN, coarse[g] * tables + fine[g]).astype(jnp.float32) for g in groups], axis=0)
+
+    def swap():
+        rows = pl.ds(first, share)
+        return pltpu.make_async_remote_copy(
+            src_ref=tally.at[rows], dst_ref=tally.at[rows],
+            send_sem=swap_sem.at[0], recv_sem=swap_sem.at[1],
+            device_id={"tm": me + 1 - 2 * core}, device_id_type=MESH,
+        )
+
+    swap().start()
+    close_round(0)
+    open_round(1)
+    fir(EDGE, frames // 2)
+    transform(frames // 2, spread_out, EDGE, 1.0)
+    close_round(1)
+    open_round(2)
+
+    swap().wait_recv()
+    total = tally[...]
     turned = jnp.concatenate([total, jnp.zeros((LANES - trials, LANES), jnp.float32)], axis=0).T
     rows_kept = blockno.shape[0]
     near_side = lax.broadcasted_iota(jnp.int32, (rows_kept, LANES), 1) < trials
@@ -278,8 +299,6 @@
     ).astype(jnp.int32)
     blockno[...] = total >> 8
     within[...] = (total & (wide - 1)).astype(jnp.float32)
-    close_round(1)
-    open_round(2)
     order = lax.broadcasted_iota(jnp.int32, (wide, LANES), 0)
     order = ((order & (RADIX - 1)) * RADIX + (order >> 4)).astype(jnp.float32)
 
@@ -351,6 +370,8 @@
         ended = jnp.logical_not(from_before) & (me == count - 1)
         transform(EDGE, spread_out, begin, jnp.where(ended, 0.0, 1.0))
 
+    close_round(2)
+    open_round(3)
     dedisperse(spread_out, frames, 0)
     height = HALF + frames + EDGE
     total = acc[0, 0:height]
@@ -397,10 +418,6 @@
     def _():
         up().start()
 
-    for i in range(2, len(rounds)):
-        close_round(i)
-        open_round(i + 1)
-
     @pl.when(me == 0)
     def _():
         risen[...] = jnp.zeros_like(risen)
@@ -422,47 +439,52 @@
     for k in range(1, reach + 1):
         series = series + landed[k - 1]
     series = series + jnp.concatenate([risen[...], jnp.zeros((half - EDGE, LANES), jnp.float32)], axis=0)
-    lane = lax.broadcasted_iota(jnp.int32, (1, LANES), 1)
+    turned = pltpu.roll(series, trials, 1)
 
     def fold(value, op):
         return op(value, pltpu.roll(value, trials, 1))
 
-    def low_half(value):
-        return jnp.where(lane < trials, value, pltpu.roll(value, trials, 1))
-
-    def high_half(value):
-        return jnp.where(lane < trials, pltpu.roll(value, trials, 1), value)
-
-    mean = fold(jnp.sum(series, axis=0, keepdims=True), jnp.add) * (1.0 / frames)
-    away = series - mean
-    spread = fold(jnp.sum(away * away, axis=0, keepdims=True), jnp.add)
+    piece = jnp.sum(series, axis=0, keepdims=True) * (1.0 / half)
+    away = series - piece
+    opposite = pltpu.roll(piece, trials, 1)
+    mean = (piece + opposite) * 0.5
+    gap = piece - opposite
+    spread = fold(jnp.sum(away * away, axis=0, keepdims=True), jnp.add) + (0.5 * half) * (gap * gap)
     peak = fold(jnp.max(series, axis=0, keepdims=True), jnp.maximum)
-    mine[...] = jnp.concatenate([jnp.where(lane < trials, mean, spread), peak], axis=0)
+    mine[...] = jnp.concatenate([mean, spread, peak, peak], axis=0)
+
+    def flipped(k):
+        place = me
+        for bit in range(count.bit_length()):
+            if k >> bit & 1:
+                place = place + (1 << bit) * (1 - 2 * lax.rem(lax.div(me, 1 << bit), 2))
+        return place
 
     def far(k):
         return pltpu.make_async_remote_copy(
             src_ref=mine, dst_ref=gathered.at[k - 1],
             send_sem=far_send.at[k - 1], recv_sem=far_recv.at[k - 1],
-            device_id={"tm": lax.rem(me + k, count)}, device_id_type=MESH,
+            device_id={"tm": flipped(k)}, device_id_type=MESH,
         )
 
-    for k in range(1, count):
+    for i in range(3, len(rounds)):
+        close_round(i)
+        open_round(i + 1)
+    for k in range(count - 1, 0, -1):
         far(k).start()
     live = jnp.maximum(jnp.sum(mask_ref[...].astype(jnp.float32)), 1.0)
     for k in range(1, count):
         far(k).wait_recv()
-    sums = gathered[:, 0, :]
-    tops = gathered[:, 1, :]
-    average = (mean + low_half(jnp.sum(sums, axis=0, keepdims=True))) * (1.0 / count)
-    offset = sums - average
-    squares = spread + high_half(jnp.sum(sums, axis=0, keepdims=True))
-    between = (mean - average) * (mean - average) + low_half(jnp.sum(offset * offset, axis=0, keepdims=True))
+    means, spreads, peaks = gathered[:, 0, :], gathered[:, 1, :], gathered[:, 2, :]
+    average = (mean + jnp.sum(means, axis=0, keepdims=True)) * (1.0 / count)
+    offset = means - average
+    squares = spread + jnp.sum(spreads, axis=0, keepdims=True)
+    between = (mean - average) * (mean - average) + jnp.sum(offset * offset, axis=0, keepdims=True)
     variance = (squares + frames * between) * (1.0 / (frames * count))
-    top = jnp.maximum(peak, jnp.max(tops, axis=0, keepdims=True))
+    top = jnp.maximum(peak, jnp.max(peaks, axis=0, keepdims=True))
     deviation = jnp.sqrt(variance + 1e-05)
-    z = (series - average) / deviation
-    z_ref[0:half, :] = z[:, :trials]
-    z_ref[half:frames, :] = pltpu.roll(z, trials, 1)[:, :trials]
+    z_ref[0:half, :] = ((series - average) / deviation)[:, :trials]
+    z_ref[half:frames, :] = ((turned - average) / deviation)[:, :trials]
     stats_ref[...] = jnp.concatenate(
         [average / live, deviation / live, (top - average) / deviation], axis=0
     )[:, :trials]
@@ -476,6 +498,7 @@
     def _():
         backward().wait_send()
 
+    swap().wait_send()
     for k in range(1, reach + 1):
         @pl.when(me >= k)
         def _():
@@ -524,7 +547,7 @@
             pltpu.VMEM((TAPS, PITCH, LANES), jnp.float32),
             pltpu.VMEM((2, RADIX, LANES), jnp.float32),
             pltpu.VMEM((2, 2 * LANES, 2 * LANES), jnp.bfloat16),
-            pltpu.VMEM((trials, NCHAN), jnp.int32),
+            pltpu.VMEM((trials // 2, NCHAN), jnp.int32),
             pltpu.VMEM((RADIX, LANES), jnp.int32),
             pltpu.VMEM((2, past - EDGE, lines, LANES), jnp.bfloat16),
             pltpu.VMEM((2, EDGE, lines, LANES), jnp.bfloat16),
@@ -533,14 +556,15 @@
             pltpu.VMEM((RADIX * frames, 2 * LANES), jnp.float32),
             pltpu.VMEM((blocks, frames, 2 * LANES), jnp.float32),
             pltpu.VMEM((blocks, EDGE, 2 * LANES), jnp.float32),
+            pltpu.VMEM((trials, LANES), jnp.float32),
             pltpu.VMEM((steps + 6, LANES), jnp.int32),
             pltpu.VMEM((steps + 6, LANES), jnp.float32),
             pltpu.VMEM((8, HALF + frames + 2 * EDGE, LANES), jnp.float32),
             pltpu.VMEM(((reach + 1) * half + EDGE, LANES), jnp.float32),
             pltpu.VMEM((reach, half, LANES), jnp.float32),
             pltpu.VMEM((EDGE, LANES), jnp.float32),
-            pltpu.VMEM((2, LANES), jnp.float32),
-            pltpu.VMEM((count - 1, 2, LANES), jnp.float32),
+            pltpu.VMEM((4, LANES), jnp.float32),
+            pltpu.VMEM((count - 1, 4, LANES), jnp.float32),
             dma((6,)),
             dma((2,)),
             dma((2,)),
@@ -548,6 +572,7 @@
             dma((reach + 1,)),
             dma((count - 1,)),
             dma((count - 1,)),
+            dma((2,)),
             pltpu.SemaphoreType.REGULAR((8,)),
         ],
         compiler_params=pltpu.CompilerParams(collective_id=1, vmem_limit_bytes=GRANT, has_side_effects=True),

time: 20.2 us -> 19.9 us (0.985)
  Pallas kernels: 19.4 us -> 19.1 us
    pallas_call x1, Pallas kernels: 18.8 us -> 18.5 us  [per_device(): pl.pallas_call(functools.partial(beam_kernel, count, frames, trials), out...]
where the time goes in v5:
time: 19.9 us; the launch traced here: 19.8 us
  Pallas kernels  19.1 us (96%)
  between operations  0.64 us (3%)
    pallas_call x1, Pallas kernels, per_device(): pl.pallas_call(functools.partial(beam_kernel, count, frames, trials), out...  18.5 us
    pallas_call x1, Pallas kernels, per_device(): pl.pallas_call(finish_kernel, out_shape=outputs, in_specs=[vmem] * 2, out...  0.63 us

profile of v5, /device:TPU:0, one launch (start us, length us, event | category | flops | bytes accessed | tf_op | source)
XLA Modules:
  0.0 19.8 jit_solution(14788516655113491870)
XLA Ops:
  0.6 18.5 %beam.1 = (f32[32,64]{1,0:T(8,128)S(1)}, f32[3,64]{1,0:T(4,128)S(1)}) custom-call(bf16[2,32,32,128]{3,2,1,0:T(8,128)(2,1)} %bitcast.7, f32[16,32,128]{2,1,0:T(8,128)} %constant.6.clone.taps_hbm, f32[2,16,128]{2,1,0:T(8,128)} %constant.7.clone.twid_hbm, bf16[2,256,256]{2,1,0:T(8,128)(2,1)} %constant.8.clone.table_hbm, s32[64,2048]{1,0:T(8,128)} %delay_hbm.1, ...), custom_call_target="tpu_custom_call" | custom-call | tf_op jit(solution)/shard_map/beam/pallas_call | solution.py:540
  19.2 0.6 %finish.1 = (f32[32,64]{1,0:T(8,128)}, f32[3,64]{1,0:T(4,128)}) custom-call(f32[32,64]{1,0:T(8,128)S(1)} %get-tuple-element.6.z_ref, f32[3,64]{1,0:T(4,128)S(1)} %get-tuple-element.7.stats_ref), custom_call_target="tpu_custom_call" | custom-call | tf_op jit(solution)/shard_map/finish/pallas_call | solution.py:581

commit v6 on v5

--- a/solution.py
+++ b/solution.py
@@ -111,7 +111,7 @@
     def number(distances):
         return sum(jnp.where(here(k), 1, 0) for k in distances)
 
-    close = (-1, 1)
+    close = (-2, -1, 1, 2)
     for k in close:
         tell(barrier, k)
     pairs = ((volt_hbm, volt_ref), (taps_hbm, taps_ref.at[:, pl.ds(0, lines)]), (delay_hbm.at[pl.ds(first, share)], delay_ref), (twid_hbm, twid_ref),
@@ -150,7 +150,7 @@
         forward().start()
 
     rounds = []
-    known = 1
+    known = 2
     while known < count - 1:
         rounds.append(known)
         known *= 2
@@ -178,7 +178,7 @@
         high = jnp.take_along_axis(odd, place, axis=1, mode="promise_in_bounds")
         usable.append(jnp.where((row & 8) == 0, low, high).astype(jnp.float32))
 
-    def fir(begin, size):
+    def fir(begin, size, base, whole):
         for part_index in range(lines // 8):
             rows = pl.ds(8 * part_index, 8)
             taps = [taps_ref[j, rows, :] for j in range(TAPS)]
@@ -193,7 +193,7 @@
                                 term = taps[i - f] * sample
                                 sums[f] = term if sums[f] is None else sums[f] + term
                     for f in range(4):
-                        start = pl.multiple_of((p * size + 4 * g + f) * PITCH, 8) + 8 * part_index
+                        start = pl.multiple_of((p * whole + base + 4 * g + f) * PITCH, 8) + 8 * part_index
                         weighted[pl.ds(start, 8), :] = sums[f]
                 return carry
 
@@ -238,6 +238,42 @@
             for b in range(blocks):
                 out[b, pl.ds(begin, size), h * LANES:(h + 1) * LANES] = parts[b] * (usable[h][b:b + 1] * scale)
 
+    def swap():
+        rows = pl.ds(first, share)
+        return pltpu.make_async_remote_copy(
+            src_ref=tally.at[rows], dst_ref=tally.at[rows],
+            send_sem=swap_sem.at[0], recv_sem=swap_sem.at[1],
+            device_id={"tm": me + 1 - 2 * core}, device_id_type=MESH,
+        )
+
+    def admit(from_before):
+        @pl.when(from_before & (me > 0))
+        def _():
+            forward().wait_recv()
+            for p in range(2):
+                ext[p, EDGE:own, 0:lines] = before[p].astype(jnp.float32)
+
+        @pl.when(jnp.logical_not(from_before) & (me < count - 1))
+        def _():
+            backward().wait_recv()
+            for p in range(2):
+                ext[p, own + frames:own + frames + EDGE, 0:lines] = after[p].astype(jnp.float32)
+
+    @pl.when(me == 0)
+    def _():
+        for p in range(2):
+            ext[p, 0:own, 0:lines] = jnp.zeros((own, lines, LANES), jnp.float32)
+
+    @pl.when(me == count - 1)
+    def _():
+        for p in range(2):
+            ext[p, own + frames:own + frames + EDGE, 0:lines] = jnp.zeros((EDGE, lines, LANES), jnp.float32)
+
+    inner = frames - 2 * EDGE
+    fir(EDGE, inner, core * EDGE, frames - EDGE)
+    admit(core == 1)
+    fir((1 - core) * (frames - EDGE), EDGE, (1 - core) * inner, frames - EDGE)
+    begin = pl.multiple_of(EDGE - core * EDGE, EDGE)
     level = lax.broadcasted_iota(jnp.int32, (8, LANES), 1)
 
     def look(table, place):
@@ -273,22 +309,16 @@
     tally[pl.ds(first, share), :] = jnp.concatenate(
         [jnp.where(level == 0, NCHAN, coarse[g] * tables + fine[g]).astype(jnp.float32) for g in groups], axis=0)
 
-    def swap():
-        rows = pl.ds(first, share)
-        return pltpu.make_async_remote_copy(
-            src_ref=tally.at[rows], dst_ref=tally.at[rows],
-            send_sem=swap_sem.at[0], recv_sem=swap_sem.at[1],
-            device_id={"tm": me + 1 - 2 * core}, device_id_type=MESH,
-        )
-
+    transform(frames - EDGE, spread_out, begin, 1.0)
     swap().start()
     close_round(0)
     open_round(1)
-    fir(EDGE, frames // 2)
-    transform(frames // 2, spread_out, EDGE, 1.0)
-    close_round(1)
-    open_round(2)
-
+    acc[...] = jnp.zeros_like(acc)
+
+    admit(core == 0)
+    begin = pl.multiple_of(core * (frames - EDGE), EDGE)
+    fir(begin, EDGE, 0, EDGE)
+    transform(EDGE, spread_out, begin, jnp.where(me == count - 1, 0.0, 1.0))
     swap().wait_recv()
     total = tally[...]
     turned = jnp.concatenate([total, jnp.zeros((LANES - trials, LANES), jnp.float32)], axis=0).T
@@ -307,8 +337,6 @@
     def pick(j):
         end = jnp.broadcast_to(within[j:j + 1, :], (wide, LANES)).astype(jnp.bfloat16)
         return jnp.minimum(jnp.maximum(end - order, jnp.zeros_like(end)), jnp.ones_like(end))
-
-    acc[...] = jnp.zeros_like(acc)
 
     def dedisperse(source, size, offset):
         values = jnp.concatenate([source[b] for b in range(blocks)], axis=0).astype(jnp.bfloat16)
@@ -339,39 +367,10 @@
 
     @pl.when(me == 0)
     def _():
-        for p in range(2):
-            ext[p, 0:own, 0:lines] = jnp.zeros((own, lines, LANES), jnp.float32)
-        fir(-EDGE, EDGE)
+        fir(-EDGE, EDGE, 0, EDGE)
         transform(EDGE, early, 0, 1.0)
         dedisperse(early, EDGE, -EDGE)
 
-    for i in range(2):
-        from_before = lax.rem(me + i, 2) == 1
-        begin = pl.multiple_of(jnp.where(from_before, 0, frames - EDGE), EDGE)
-
-        @pl.when(from_before & (me > 0))
-        def _():
-            forward().wait_recv()
-            for p in range(2):
-                ext[p, EDGE:own, 0:lines] = before[p].astype(jnp.float32)
-
-        @pl.when(jnp.logical_not(from_before) & (me < count - 1))
-        def _():
-            backward().wait_recv()
-            for p in range(2):
-                ext[p, own + frames:own + frames + EDGE, 0:lines] = after[p].astype(jnp.float32)
-
-        @pl.when(jnp.logical_not(from_before) & (me == count - 1))
-        def _():
-            for p in range(2):
-                ext[p, own + frames:own + frames + EDGE, 0:lines] = jnp.zeros((EDGE, lines, LANES), jnp.float32)
-
-        fir(begin, EDGE)
-        ended = jnp.logical_not(from_before) & (me == count - 1)
-        transform(EDGE, spread_out, begin, jnp.where(ended, 0.0, 1.0))
-
-    close_round(2)
-    open_round(3)
     dedisperse(spread_out, frames, 0)
     height = HALF + frames + EDGE
     total = acc[0, 0:height]
@@ -418,6 +417,9 @@
     def _():
         up().start()
 
+    close_round(1)
+    open_round(2)
+
     @pl.when(me == 0)
     def _():
         risen[...] = jnp.zeros_like(risen)
@@ -467,7 +469,7 @@
             device_id={"tm": flipped(k)}, device_id_type=MESH,
         )
 
-    for i in range(3, len(rounds)):
+    for i in range(2, len(rounds)):
         close_round(i)
         open_round(i + 1)
     for k in range(count - 1, 0, -1):
@@ -552,8 +554,8 @@
             pltpu.VMEM((2, past - EDGE, lines, LANES), jnp.bfloat16),
             pltpu.VMEM((2, EDGE, lines, LANES), jnp.bfloat16),
             pltpu.VMEM((2, frames + past + EDGE, PITCH, LANES), jnp.float32),
-            pltpu.VMEM((frames * PITCH, LANES), jnp.float32),
-            pltpu.VMEM((RADIX * frames, 2 * LANES), jnp.float32),
+            pltpu.VMEM((2 * frames * PITCH, LANES), jnp.float32),
+            pltpu.VMEM((2 * RADIX * frames, 2 * LANES), jnp.float32),
             pltpu.VMEM((blocks, frames, 2 * LANES), jnp.float32),
             pltpu.VMEM((blocks, EDGE, 2 * LANES), jnp.float32),
             pltpu.VMEM((trials, LANES), jnp.float32),

time: 19.9 us -> 20.1 us (1.010)
  no operation moved by 1% of the time
where the time goes in v6:
time: 20.1 us; the launch traced here: 20 us
  Pallas kernels  19.3 us (96%)
  between operations  0.64 us (3%)
    pallas_call x1, Pallas kernels, per_device(): pl.pallas_call(functools.partial(beam_kernel, count, frames, trials), out...  18.7 us
    pallas_call x1, Pallas kernels, per_device(): pl.pallas_call(finish_kernel, out_shape=outputs, in_specs=[vmem] * 2, out...  0.63 us

profile of v6, /device:TPU:0, one launch (start us, length us, event | category | flops | bytes accessed | tf_op | source)
XLA Modules:
  0.0 20.0 jit_solution(13444721476573787647)
XLA Ops:
  0.6 18.7 %beam.1 = (f32[32,64]{1,0:T(8,128)S(1)}, f32[3,64]{1,0:T(4,128)S(1)}) custom-call(bf16[2,32,32,128]{3,2,1,0:T(8,128)(2,1)} %bitcast.7, f32[16,32,128]{2,1,0:T(8,128)} %constant.6.clone.taps_hbm, f32[2,16,128]{2,1,0:T(8,128)} %constant.7.clone.twid_hbm, bf16[2,256,256]{2,1,0:T(8,128)(2,1)} %constant.8.clone.table_hbm, s32[64,2048]{1,0:T(8,128)} %delay_hbm.1, ...), custom_call_target="tpu_custom_call" | custom-call | tf_op jit(solution)/shard_map/beam/pallas_call | solution.py:542
  19.3 0.6 %finish.1 = (f32[32,64]{1,0:T(8,128)}, f32[3,64]{1,0:T(4,128)}) custom-call(f32[32,64]{1,0:T(8,128)S(1)} %get-tuple-element.6.z_ref, f32[3,64]{1,0:T(4,128)S(1)} %get-tuple-element.7.stats_ref), custom_call_target="tpu_custom_call" | custom-call | tf_op jit(solution)/shard_map/finish/pallas_call | solution.py:583

commit v7 on v6

--- a/solution.py
+++ b/solution.py
@@ -83,7 +83,7 @@
 
 
 def beam_kernel(count, frames, trials, volt_hbm, taps_hbm, twid_hbm, table_hbm, delay_hbm, mask_hbm, z_ref, stats_ref,
-                volt_ref, taps_ref, twid_ref, table_ref, delay_ref, mask_ref, before, after, ext, weighted, sections,
+                volt_ref, taps_ref, twid_ref, table_ref, delay_ref, mask_ref, before, after, ext, weighted, held, sections,
                 spread_out, early, tally, blockno, within, acc, part, landed, risen, mine, gathered,
                 load_sem, halo_send, halo_recv, near_send, near_recv, far_send, far_recv, swap_sem, know):
     me = lax.axis_index("tm")
@@ -95,6 +95,9 @@
     wide = NCHAN // blocks
     reach = MAXD // frames
     steps = HALF + 2
+    steps_of = [
+        (1 << bit) * (1 - 2 * lax.rem(lax.div(me, 1 << bit), 2)) for bit in range((count - 1).bit_length())
+    ]
     share = trials // 2
     core = lax.rem(me, 2)
     first = pl.multiple_of(core * share, share)
@@ -111,7 +114,7 @@
     def number(distances):
         return sum(jnp.where(here(k), 1, 0) for k in distances)
 
-    close = (-2, -1, 1, 2)
+    close = (-1, 1)
     for k in close:
         tell(barrier, k)
     pairs = ((volt_hbm, volt_ref), (taps_hbm, taps_ref.at[:, pl.ds(0, lines)]), (delay_hbm.at[pl.ds(first, share)], delay_ref), (twid_hbm, twid_ref),
@@ -132,25 +135,35 @@
             send_sem=halo_send.at[1], recv_sem=halo_recv.at[1], device_id={"tm": me - 1}, device_id_type=MESH,
         )
 
+    @pl.when(core == 0)
+    def _():
+        for p in range(2):
+            ext[p, 0:own, 0:lines] = jnp.zeros((own, lines, LANES), jnp.float32)
+
+    @pl.when(core == 1)
+    def _():
+        for p in range(2):
+            ext[p, own + frames:own + frames + EDGE, 0:lines] = jnp.zeros((EDGE, lines, LANES), jnp.float32)
+
     loads[0].wait()
+    wait_some(barrier, number(close))
+
+    @pl.when((core == 1) & (me < count - 1))
+    def _():
+        forward().start()
+
+    @pl.when(me > 0)
+    def _():
+        backward().start()
+
+    @pl.when((core == 0) & (me < count - 1))
+    def _():
+        forward().start()
+
     for p in range(2):
         ext[p, own:own + frames, 0:lines] = volt_ref[p].astype(jnp.float32)
-    wait_some(barrier, number(close))
-
-    @pl.when((core == 1) & (me < count - 1))
-    def _():
-        forward().start()
-
-    @pl.when(me > 0)
-    def _():
-        backward().start()
-
-    @pl.when((core == 0) & (me < count - 1))
-    def _():
-        forward().start()
-
     rounds = []
-    known = 2
+    known = 1
     while known < count - 1:
         rounds.append(known)
         known *= 2
@@ -178,7 +191,7 @@
         high = jnp.take_along_axis(odd, place, axis=1, mode="promise_in_bounds")
         usable.append(jnp.where((row & 8) == 0, low, high).astype(jnp.float32))
 
-    def fir(begin, size, base, whole):
+    def fir(begin, size, out):
         for part_index in range(lines // 8):
             rows = pl.ds(8 * part_index, 8)
             taps = [taps_ref[j, rows, :] for j in range(TAPS)]
@@ -193,13 +206,29 @@
                                 term = taps[i - f] * sample
                                 sums[f] = term if sums[f] is None else sums[f] + term
                     for f in range(4):
-                        start = pl.multiple_of((p * whole + base + 4 * g + f) * PITCH, 8) + 8 * part_index
-                        weighted[pl.ds(start, 8), :] = sums[f]
+                        start = pl.multiple_of((p * size + 4 * g + f) * PITCH, 8) + 8 * part_index
+                        out[pl.ds(start, 8), :] = sums[f]
                 return carry
 
             lax.fori_loop(0, size // 4, some, 0)
 
-    def transform(size, out, begin, scale):
+    def rest(w0, low, high):
+        for part_index in range(lines // 8):
+            rows = pl.ds(8 * part_index, 8)
+            for p in range(2):
+                sums = {}
+                for row in range(low, high):
+                    sample = ext[p, row, rows, :]
+                    for f in range(EDGE):
+                        j = row - EDGE - w0 - f
+                        if 0 <= j < TAPS:
+                            term = taps_ref[j, rows, :] * sample
+                            sums[f] = term if f not in sums else sums[f] + term
+                for f, value in sums.items():
+                    start = (p * EDGE + f) * PITCH + 8 * part_index
+                    held[start:start + 8, :] = held[start:start + 8, :] + value
+
+    def transform(size, out, begin, scale, weighted):
         group = 8
         rows_half = 2 * size
         for g in range(rows_half // group):
@@ -259,21 +288,8 @@
             for p in range(2):
                 ext[p, own + frames:own + frames + EDGE, 0:lines] = after[p].astype(jnp.float32)
 
-    @pl.when(me == 0)
-    def _():
-        for p in range(2):
-            ext[p, 0:own, 0:lines] = jnp.zeros((own, lines, LANES), jnp.float32)
-
-    @pl.when(me == count - 1)
-    def _():
-        for p in range(2):
-            ext[p, own + frames:own + frames + EDGE, 0:lines] = jnp.zeros((EDGE, lines, LANES), jnp.float32)
-
     inner = frames - 2 * EDGE
-    fir(EDGE, inner, core * EDGE, frames - EDGE)
-    admit(core == 1)
-    fir((1 - core) * (frames - EDGE), EDGE, (1 - core) * inner, frames - EDGE)
-    begin = pl.multiple_of(EDGE - core * EDGE, EDGE)
+    fir(EDGE, inner, weighted)
     level = lax.broadcasted_iota(jnp.int32, (8, LANES), 1)
 
     def look(table, place):
@@ -309,16 +325,18 @@
     tally[pl.ds(first, share), :] = jnp.concatenate(
         [jnp.where(level == 0, NCHAN, coarse[g] * tables + fine[g]).astype(jnp.float32) for g in groups], axis=0)
 
-    transform(frames - EDGE, spread_out, begin, 1.0)
+    transform(inner, spread_out, EDGE, 1.0, weighted)
     swap().start()
     close_round(0)
     open_round(1)
+    late_begin = pl.multiple_of(core * (frames - EDGE), EDGE)
+    fir(late_begin, EDGE, held)
+    admit(core == 1)
+    begin = pl.multiple_of((1 - core) * (frames - EDGE), EDGE)
+    fir(begin, EDGE, weighted)
+    transform(EDGE, spread_out, begin, 1.0, weighted)
     acc[...] = jnp.zeros_like(acc)
 
-    admit(core == 0)
-    begin = pl.multiple_of(core * (frames - EDGE), EDGE)
-    fir(begin, EDGE, 0, EDGE)
-    transform(EDGE, spread_out, begin, jnp.where(me == count - 1, 0.0, 1.0))
     swap().wait_recv()
     total = tally[...]
     turned = jnp.concatenate([total, jnp.zeros((LANES - trials, LANES), jnp.float32)], axis=0).T
@@ -367,10 +385,23 @@
 
     @pl.when(me == 0)
     def _():
-        fir(-EDGE, EDGE, 0, EDGE)
-        transform(EDGE, early, 0, 1.0)
+        fir(-EDGE, EDGE, weighted)
+        transform(EDGE, early, 0, 1.0, weighted)
         dedisperse(early, EDGE, -EDGE)
 
+    admit(core == 0)
+
+    @pl.when(core == 0)
+    def _():
+        rest(0, EDGE, own)
+
+    @pl.when(core == 1)
+    def _():
+        rest(frames - EDGE, own + frames, own + frames + EDGE)
+
+    transform(EDGE, spread_out, late_begin, jnp.where(me == count - 1, 0.0, 1.0), held)
+    close_round(1)
+    open_round(2)
     dedisperse(spread_out, frames, 0)
     height = HALF + frames + EDGE
     total = acc[0, 0:height]
@@ -417,8 +448,8 @@
     def _():
         up().start()
 
-    close_round(1)
-    open_round(2)
+    close_round(2)
+    open_round(3)
 
     @pl.when(me == 0)
     def _():
@@ -457,9 +488,9 @@
 
     def flipped(k):
         place = me
-        for bit in range(count.bit_length()):
+        for bit, step in enumerate(steps_of):
             if k >> bit & 1:
-                place = place + (1 << bit) * (1 - 2 * lax.rem(lax.div(me, 1 << bit), 2))
+                place = place + step
         return place
 
     def far(k):
@@ -469,7 +500,7 @@
             device_id={"tm": flipped(k)}, device_id_type=MESH,
         )
 
-    for i in range(2, len(rounds)):
+    for i in range(3, len(rounds)):
         close_round(i)
         open_round(i + 1)
     for k in range(count - 1, 0, -1):
@@ -555,6 +586,7 @@
             pltpu.VMEM((2, EDGE, lines, LANES), jnp.bfloat16),
             pltpu.VMEM((2, frames + past + EDGE, PITCH, LANES), jnp.float32),
             pltpu.VMEM((2 * frames * PITCH, LANES), jnp.float32),
+            pltpu.VMEM((2 * EDGE * PITCH, LANES), jnp.float32),
             pltpu.VMEM((2 * RADIX * frames, 2 * LANES), jnp.float32),
             pltpu.VMEM((blocks, frames, 2 * LANES), jnp.float32),
             pltpu.VMEM((blocks, EDGE, 2 * LANES), jnp.float32),

time: 20.1 us -> 19.8 us (0.985)
  Pallas kernels: 19.3 us -> 19 us
    pallas_call x1, Pallas kernels: 18.7 us -> 18.3 us  [per_device(): pl.pallas_call(functools.partial(beam_kernel, count, frames, trials), out...]
where the time goes in v7:
time: 19.8 us; the launch traced here: 19.6 us
  Pallas kernels  19 us (96%)
  between operations  0.64 us (3%)
    pallas_call x1, Pallas kernels, per_device(): pl.pallas_call(functools.partial(beam_kernel, count, frames, trials), out...  18.3 us
    pallas_call x1, Pallas kernels, per_device(): pl.pallas_call(finish_kernel, out_shape=outputs, in_specs=[vmem] * 2, out...  0.63 us

profile of v7, /device:TPU:0, one launch (start us, length us, event | category | flops | bytes accessed | tf_op | source)
XLA Modules:
  0.0 19.6 jit_solution(1278536033683859458)
XLA Ops:
  0.6 18.3 %beam.1 = (f32[32,64]{1,0:T(8,128)S(1)}, f32[3,64]{1,0:T(4,128)S(1)}) custom-call(bf16[2,32,32,128]{3,2,1,0:T(8,128)(2,1)} %bitcast.7, f32[16,32,128]{2,1,0:T(8,128)} %constant.6.clone.taps_hbm, f32[2,16,128]{2,1,0:T(8,128)} %constant.7.clone.twid_hbm, bf16[2,256,256]{2,1,0:T(8,128)(2,1)} %constant.8.clone.table_hbm, s32[64,2048]{1,0:T(8,128)} %delay_hbm.1, ...), custom_call_target="tpu_custom_call" | custom-call | tf_op jit(solution)/shard_map/beam/pallas_call | solution.py:573
  19.0 0.6 %finish.1 = (f32[32,64]{1,0:T(8,128)}, f32[3,64]{1,0:T(4,128)}) custom-call(f32[32,64]{1,0:T(8,128)S(1)} %get-tuple-element.6.z_ref, f32[3,64]{1,0:T(4,128)S(1)} %get-tuple-element.7.stats_ref), custom_call_target="tpu_custom_call" | custom-call | tf_op jit(solution)/shard_map/finish/pallas_call | solution.py:615

commit v8 on v7

--- a/solution.py
+++ b/solution.py
@@ -94,7 +94,6 @@
     blocks = LANES // RADIX
     wide = NCHAN // blocks
     reach = MAXD // frames
-    steps = HALF + 2
     steps_of = [
         (1 << bit) * (1 - 2 * lax.rem(lax.div(me, 1 << bit), 2)) for bit in range((count - 1).bit_length())
     ]
@@ -178,18 +177,7 @@
             wait_some(know.at[i], number((-rounds[i], rounds[i])))
 
     open_round(0)
-    for load in loads[1:]:
-        load.wait()
-
-    row = lax.broadcasted_iota(jnp.int32, (blocks, LANES), 1)
-    even = mask_ref[pl.ds(0, blocks, stride=2), :]
-    odd = mask_ref[pl.ds(1, blocks, stride=2), :]
-    usable = []
-    for h in range(2):
-        place = (row & 7) * RADIX + 8 * h + (row >> 4)
-        low = jnp.take_along_axis(even, place, axis=1, mode="promise_in_bounds")
-        high = jnp.take_along_axis(odd, place, axis=1, mode="promise_in_bounds")
-        usable.append(jnp.where((row & 8) == 0, low, high).astype(jnp.float32))
+    loads[1].wait()
 
     def fir(begin, size, out):
         for part_index in range(lines // 8):
@@ -210,7 +198,7 @@
                         out[pl.ds(start, 8), :] = sums[f]
                 return carry
 
-            lax.fori_loop(0, size // 4, some, 0)
+            lax.fori_loop(0, size // 4, some, 0, unroll=2)
 
     def rest(w0, low, high):
         for part_index in range(lines // 8):
@@ -257,13 +245,24 @@
         chunk = lax.broadcasted_iota(jnp.int32, (size, LANES), 1) >> 4
         for h in range(2):
             parts = [energy[8 * h + i] for i in range(8)]
-            for bit in (4, 2, 1):
-                kept = (chunk & bit) == 0
-                for i in range(8):
-                    if i & bit == 0:
-                        low_part, high_part = parts[i], parts[i | bit]
-                        parts[i] = jnp.where(kept, low_part, pltpu.roll(high_part, bit * RADIX, 1))
-                        parts[i | bit] = jnp.where(kept, pltpu.roll(low_part, LANES - bit * RADIX, 1), high_part)
+            if size > EDGE:
+                for bit in (4, 2, 1):
+                    kept = (chunk & bit) == 0
+                    for i in range(8):
+                        if i & bit == 0:
+                            low_part, high_part = parts[i], parts[i | bit]
+                            parts[i] = jnp.where(kept, low_part, pltpu.roll(high_part, bit * RADIX, 1))
+                            parts[i | bit] = jnp.where(kept, pltpu.roll(low_part, LANES - bit * RADIX, 1), high_part)
+            else:
+                moved = []
+                for b in range(blocks):
+                    mixed = parts[b]
+                    for i in range(blocks):
+                        if i != b:
+                            turned = pltpu.roll(parts[i], (i - b) % blocks * RADIX, 1)
+                            mixed = jnp.where(chunk == i, turned, mixed)
+                    moved.append(mixed)
+                parts = moved
             for b in range(blocks):
                 out[b, pl.ds(begin, size), h * LANES:(h + 1) * LANES] = parts[b] * (usable[h][b:b + 1] * scale)
 
@@ -290,6 +289,18 @@
 
     inner = frames - 2 * EDGE
     fir(EDGE, inner, weighted)
+    for load in loads[2:]:
+        load.wait()
+    row = lax.broadcasted_iota(jnp.int32, (blocks, LANES), 1)
+    even = mask_ref[pl.ds(0, blocks, stride=2), :]
+    odd = mask_ref[pl.ds(1, blocks, stride=2), :]
+    usable = []
+    for h in range(2):
+        place = (row & 7) * RADIX + 8 * h + (row >> 4)
+        low = jnp.take_along_axis(even, place, axis=1, mode="promise_in_bounds")
+        high = jnp.take_along_axis(odd, place, axis=1, mode="promise_in_bounds")
+        usable.append(jnp.where((row & 8) == 0, low, high).astype(jnp.float32))
+
     level = lax.broadcasted_iota(jnp.int32, (8, LANES), 1)
 
     def look(table, place):
@@ -339,12 +350,10 @@
 
     swap().wait_recv()
     total = tally[...]
-    turned = jnp.concatenate([total, jnp.zeros((LANES - trials, LANES), jnp.float32)], axis=0).T
+    turned = jnp.concatenate([total, total], axis=0).T
     rows_kept = blockno.shape[0]
     near_side = lax.broadcasted_iota(jnp.int32, (rows_kept, LANES), 1) < trials
-    total = jnp.where(
-        near_side, turned[0:rows_kept], pltpu.roll(turned[HALF:HALF + rows_kept], trials, 1)
-    ).astype(jnp.int32)
+    total = jnp.where(near_side, turned[0:rows_kept], turned[HALF:HALF + rows_kept]).astype(jnp.int32)
     blockno[...] = total >> 8
     within[...] = (total & (wide - 1)).astype(jnp.float32)
     order = lax.broadcasted_iota(jnp.int32, (wide, LANES), 0)
@@ -364,24 +373,33 @@
         prefix = jnp.zeros((size, LANES), jnp.float32)
         for b in range(blocks):
             prefix = prefix + jnp.where(column > b, sums[b * size:(b + 1) * size], 0.0)
+        near_side = column < trials
+
+        def add(j, change):
+            a, m = divmod(j, 8)
+            place = HALF + EDGE + offset - 8 * a
+            acc[m, place:place + size] += change
+
         last = None
-        for i in range(steps // 2):
-            found = dot(values, jnp.concatenate([pick(2 * i), pick(2 * i + 1)], axis=1))
+        for i in range(HALF // 2):
+            found = dot(values, jnp.concatenate([pick(2 * i + 1), pick(2 * i + 2)], axis=1))
             for side in range(2):
-                j = 2 * i + side
+                j = 2 * i + side + 1
                 which = jnp.broadcast_to(blockno[j:j + 1, :], (size, LANES))
                 inner = jnp.zeros((size, LANES), jnp.float32)
                 for b in range(blocks):
                     inner = jnp.where(which == b, found[b * size:(b + 1) * size, side * LANES:(side + 1) * LANES], inner)
                 now = inner + jnp.take_along_axis(prefix, which, axis=1, mode="promise_in_bounds")
-                if j:
-                    change = last - now
-                    if j - 1 == HALF:
-                        change = jnp.where(column < trials, 0.0, change)
-                    a, m = divmod(j - 1, 8)
-                    place = HALF + EDGE + offset - 8 * a
-                    acc[m, place:place + size] += change
+                if j == 1:
+                    whole = sums[0:size]
+                    for b in range(1, blocks):
+                        whole = whole + sums[b * size:(b + 1) * size]
+                    add(0, jnp.where(near_side, whole - now, 0.0))
+                    after_half = jnp.where(near_side, pltpu.roll(now, trials, 1), 0.0)
+                else:
+                    add(j - 1, last - now)
                 last = now
+        add(HALF, last - after_half)
 
     @pl.when(me == 0)
     def _():
@@ -558,7 +576,6 @@
     blocks = LANES // RADIX
     wide = NCHAN // blocks
     reach = MAXD // frames
-    steps = HALF + 2
     past = TAPS - 1
     vmem = pl.BlockSpec(memory_space=pltpu.VMEM)
     hbm = pl.BlockSpec(memory_space=pltpu.HBM)
@@ -591,8 +608,8 @@
             pltpu.VMEM((blocks, frames, 2 * LANES), jnp.float32),
             pltpu.VMEM((blocks, EDGE, 2 * LANES), jnp.float32),
             pltpu.VMEM((trials, LANES), jnp.float32),
-            pltpu.VMEM((steps + 6, LANES), jnp.int32),
-            pltpu.VMEM((steps + 6, LANES), jnp.float32),
+            pltpu.VMEM((HALF + 8, LANES), jnp.int32),
+            pltpu.VMEM((HALF + 8, LANES), jnp.float32),
             pltpu.VMEM((8, HALF + frames + 2 * EDGE, LANES), jnp.float32),
             pltpu.VMEM(((reach + 1) * half + EDGE, LANES), jnp.float32),
             pltpu.VMEM((reach, half, LANES), jnp.float32),

time: 19.8 us -> 19.6 us (0.990)
  no operation moved by 1% of the time
where the time goes in v8:
time: 19.6 us; the launch traced here: 19.5 us
  Pallas kernels  18.9 us (96%)
  between operations  0.64 us (3%)
    pallas_call x1, Pallas kernels, per_device(): pl.pallas_call(functools.partial(beam_kernel, count, frames, trials), out...  18.2 us
    pallas_call x1, Pallas kernels, per_device(): pl.pallas_call(finish_kernel, out_shape=outputs, in_specs=[vmem] * 2, out...  0.63 us

profile of v8, /device:TPU:0, one launch (start us, length us, event | category | flops | bytes accessed | tf_op | source)
XLA Modules:
  0.0 19.5 jit_solution(4354655231534537656)
XLA Ops:
  0.6 18.2 %beam.1 = (f32[32,64]{1,0:T(8,128)S(1)}, f32[3,64]{1,0:T(4,128)S(1)}) custom-call(bf16[2,32,32,128]{3,2,1,0:T(8,128)(2,1)} %bitcast.7, f32[16,32,128]{2,1,0:T(8,128)} %constant.6.clone.taps_hbm, f32[2,16,128]{2,1,0:T(8,128)} %constant.7.clone.twid_hbm, bf16[2,256,256]{2,1,0:T(8,128)(2,1)} %constant.8.clone.table_hbm, s32[64,2048]{1,0:T(8,128)} %delay_hbm.1, ...), custom_call_target="tpu_custom_call" | custom-call | tf_op jit(solution)/shard_map/beam/pallas_call | solution.py:590
  18.9 0.6 %finish.1 = (f32[32,64]{1,0:T(8,128)}, f32[3,64]{1,0:T(4,128)}) custom-call(f32[32,64]{1,0:T(8,128)S(1)} %get-tuple-element.6.z_ref, f32[3,64]{1,0:T(4,128)S(1)} %get-tuple-element.7.stats_ref), custom_call_target="tpu_custom_call" | custom-call | tf_op jit(solution)/shard_map/finish/pallas_call | solution.py:632

commit v9 on v8

--- a/solution.py
+++ b/solution.py
@@ -365,8 +365,8 @@
         end = jnp.broadcast_to(within[j:j + 1, :], (wide, LANES)).astype(jnp.bfloat16)
         return jnp.minimum(jnp.maximum(end - order, jnp.zeros_like(end)), jnp.ones_like(end))
 
-    def dedisperse(source, size, offset):
-        values = jnp.concatenate([source[b] for b in range(blocks)], axis=0).astype(jnp.bfloat16)
+    def dedisperse(source, begin, size, offset):
+        values = jnp.concatenate([source[b, begin:begin + size] for b in range(blocks)], axis=0).astype(jnp.bfloat16)
         dot = functools.partial(jnp.dot, preferred_element_type=jnp.float32)
         sums = dot(values, jnp.ones((wide, LANES), jnp.bfloat16))
         column = lax.broadcasted_iota(jnp.int32, (size, LANES), 1)
@@ -405,7 +405,11 @@
     def _():
         fir(-EDGE, EDGE, weighted)
         transform(EDGE, early, 0, 1.0, weighted)
-        dedisperse(early, EDGE, -EDGE)
+        dedisperse(early, 0, EDGE, -EDGE)
+
+    @pl.when(core == 1)
+    def _():
+        dedisperse(spread_out, 0, frames - EDGE, 0)
 
     admit(core == 0)
 
@@ -420,7 +424,14 @@
     transform(EDGE, spread_out, late_begin, jnp.where(me == count - 1, 0.0, 1.0), held)
     close_round(1)
     open_round(2)
-    dedisperse(spread_out, frames, 0)
+    @pl.when(core == 0)
+    def _():
+        dedisperse(spread_out, 0, frames, 0)
+
+    @pl.when(core == 1)
+    def _():
+        dedisperse(spread_out, frames - EDGE, EDGE, frames - EDGE)
+
     height = HALF + frames + EDGE
     total = acc[0, 0:height]
     for m in range(1, 8):

time: 19.6 us -> 19.1 us (0.974)
  Pallas kernels: 18.9 us -> 18.3 us
    pallas_call x1, Pallas kernels: 18.2 us -> 17.7 us  [per_device(): pl.pallas_call(functools.partial(beam_kernel, count, frames, trials), out...]
where the time goes in v9:
time: 19.1 us; the launch traced here: 19 us
  Pallas kernels  18.3 us (96%)
  between operations  0.64 us (3%)
    pallas_call x1, Pallas kernels, per_device(): pl.pallas_call(functools.partial(beam_kernel, count, frames, trials), out...  17.7 us
    pallas_call x1, Pallas kernels, per_device(): pl.pallas_call(finish_kernel, out_shape=outputs, in_specs=[vmem] * 2, out...  0.63 us

profile of v9, /device:TPU:0, one launch (start us, length us, event | category | flops | bytes accessed | tf_op | source)
XLA Modules:
  0.0 19.0 jit_solution(4826841429686717233)
XLA Ops:
  0.6 17.7 %beam.1 = (f32[32,64]{1,0:T(8,128)S(1)}, f32[3,64]{1,0:T(4,128)S(1)}) custom-call(bf16[2,32,32,128]{3,2,1,0:T(8,128)(2,1)} %bitcast.7, f32[16,32,128]{2,1,0:T(8,128)} %constant.6.clone.taps_hbm, f32[2,16,128]{2,1,0:T(8,128)} %constant.7.clone.twid_hbm, bf16[2,256,256]{2,1,0:T(8,128)(2,1)} %constant.8.clone.table_hbm, s32[64,2048]{1,0:T(8,128)} %delay_hbm.1, ...), custom_call_target="tpu_custom_call" | custom-call | tf_op jit(solution)/shard_map/beam/pallas_call | solution.py:601
  18.4 0.6 %finish.1 = (f32[32,64]{1,0:T(8,128)}, f32[3,64]{1,0:T(4,128)}) custom-call(f32[32,64]{1,0:T(8,128)S(1)} %get-tuple-element.6.z_ref, f32[3,64]{1,0:T(4,128)S(1)} %get-tuple-element.7.stats_ref), custom_call_target="tpu_custom_call" | custom-call | tf_op jit(solution)/shard_map/finish/pallas_call | solution.py:643

commit v10 on v9

--- a/solution.py
+++ b/solution.py
@@ -114,12 +114,13 @@
         return sum(jnp.where(here(k), 1, 0) for k in distances)
 
     close = (-1, 1)
-    for k in close:
-        tell(barrier, k)
     pairs = ((volt_hbm, volt_ref), (taps_hbm, taps_ref.at[:, pl.ds(0, lines)]), (delay_hbm.at[pl.ds(first, share)], delay_ref), (twid_hbm, twid_ref),
              (table_hbm, table_ref), (mask_hbm, mask_ref))
     loads = [pltpu.make_async_copy(a, b, load_sem.at[i]) for i, (a, b) in enumerate(pairs)]
-    for load in loads:
+    loads[0].start()
+    for k in close:
+        tell(barrier, k)
+    for load in loads[1:]:
         load.start()
 
     def forward():

time: 19.1 us -> 19.1 us (level)
  no operation moved by 1% of the time
where the time goes in v10:
time: 19.1 us; the launch traced here: 19 us
  Pallas kernels  18.3 us (96%)
  between operations  0.64 us (3%)
    pallas_call x1, Pallas kernels, per_device(): pl.pallas_call(functools.partial(beam_kernel, count, frames, trials), out...  17.7 us
    pallas_call x1, Pallas kernels, per_device(): pl.pallas_call(finish_kernel, out_shape=outputs, in_specs=[vmem] * 2, out...  0.63 us

profile of v10, /device:TPU:0, one launch (start us, length us, event | category | flops | bytes accessed | tf_op | source)
XLA Modules:
  0.0 19.0 jit_solution(15713287601446589413)
XLA Ops:
  0.6 17.7 %beam.1 = (f32[32,64]{1,0:T(8,128)S(1)}, f32[3,64]{1,0:T(4,128)S(1)}) custom-call(bf16[2,32,32,128]{3,2,1,0:T(8,128)(2,1)} %bitcast.7, f32[16,32,128]{2,1,0:T(8,128)} %constant.6.clone.taps_hbm, f32[2,16,128]{2,1,0:T(8,128)} %constant.7.clone.twid_hbm, bf16[2,256,256]{2,1,0:T(8,128)(2,1)} %constant.8.clone.table_hbm, s32[64,2048]{1,0:T(8,128)} %delay_hbm.1, ...), custom_call_target="tpu_custom_call" | custom-call | tf_op jit(solution)/shard_map/beam/pallas_call | solution.py:602
  18.4 0.6 %finish.1 = (f32[32,64]{1,0:T(8,128)}, f32[3,64]{1,0:T(4,128)}) custom-call(f32[32,64]{1,0:T(8,128)S(1)} %get-tuple-element.6.z_ref, f32[3,64]{1,0:T(4,128)S(1)} %get-tuple-element.7.stats_ref), custom_call_target="tpu_custom_call" | custom-call | tf_op jit(solution)/shard_map/finish/pallas_call | solution.py:644

commit v11 on v10

--- a/solution.py
+++ b/solution.py
@@ -131,7 +131,7 @@
 
     def backward():
         return pltpu.make_async_remote_copy(
-            src_ref=volt_ref.at[:, pl.ds(0, EDGE)], dst_ref=after,
+            src_ref=volt_hbm.at[:, pl.ds(0, EDGE)], dst_ref=after,
             send_sem=halo_send.at[1], recv_sem=halo_recv.at[1], device_id={"tm": me - 1}, device_id_type=MESH,
         )
 
@@ -145,16 +145,18 @@
         for p in range(2):
             ext[p, own + frames:own + frames + EDGE, 0:lines] = jnp.zeros((EDGE, lines, LANES), jnp.float32)
 
+    wait_some(barrier, number(close))
+
+    @pl.when(me > 0)
+    def _():
+        backward().start()
+
     loads[0].wait()
-    wait_some(barrier, number(close))
 
     @pl.when((core == 1) & (me < count - 1))
     def _():
         forward().start()
 
-    @pl.when(me > 0)
-    def _():
-        backward().start()
 
     @pl.when((core == 0) & (me < count - 1))
     def _():

time: 19.1 us -> 19 us (level)
  no operation moved by 1% of the time
where the time goes in v11:
time: 19 us; the launch traced here: 18.8 us
  Pallas kernels  18.2 us (96%)
  between operations  0.64 us (3%)
    pallas_call x1, Pallas kernels, per_device(): pl.pallas_call(functools.partial(beam_kernel, count, frames, trials), out...  17.6 us
    pallas_call x1, Pallas kernels, per_device(): pl.pallas_call(finish_kernel, out_shape=outputs, in_specs=[vmem] * 2, out...  0.63 us

profile of v11, /device:TPU:0, one launch (start us, length us, event | category | flops | bytes accessed | tf_op | source)
XLA Modules:
  0.0 18.8 jit_solution(2728866045526456890)
XLA Ops:
  0.6 17.6 %beam.1 = (f32[32,64]{1,0:T(8,128)S(1)}, f32[3,64]{1,0:T(4,128)S(1)}) custom-call(bf16[2,32,32,128]{3,2,1,0:T(8,128)(2,1)} %bitcast.7, f32[16,32,128]{2,1,0:T(8,128)} %constant.6.clone.taps_hbm, f32[2,16,128]{2,1,0:T(8,128)} %constant.7.clone.twid_hbm, bf16[2,256,256]{2,1,0:T(8,128)(2,1)} %constant.8.clone.table_hbm, s32[64,2048]{1,0:T(8,128)} %delay_hbm.1, ...), custom_call_target="tpu_custom_call" | custom-call | tf_op jit(solution)/shard_map/beam/pallas_call | solution.py:604
  18.2 0.6 %finish.1 = (f32[32,64]{1,0:T(8,128)}, f32[3,64]{1,0:T(4,128)}) custom-call(f32[32,64]{1,0:T(8,128)S(1)} %get-tuple-element.6.z_ref, f32[3,64]{1,0:T(4,128)S(1)} %get-tuple-element.7.stats_ref), custom_call_target="tpu_custom_call" | custom-call | tf_op jit(solution)/shard_map/finish/pallas_call | solution.py:646
